TPU v7x, 1024 devices: a whole 4x8x16 slice. The times are simulated.
1024 devices in a mesh: rows: 128 (over y, z), protos: 8 (over x, core).
Axes of the slice: x: 4, y: 8, z: 16, core: 2. Of those that a mesh axis runs over, the one named last changes fastest.
Arguments:
- features: bfloat16 [49152, 256], P('rows', 'protos'), may hold values from -12 to 12
- prototypes: bfloat16 [65536, 256], P('protos', 'rows'), may hold values from -8 to 8
- masked_index: int32 [24576], P('rows'), may hold values from 0 to 383
Outputs:
- targets: bfloat16 [24576, 65536], P('rows', 'protos')
Inputs may be any that keep to these rules, and one draw needn't show every extreme that they name: Row r of the whole takes patch (r // 192) * 384 + masked_index[r] of features.
All inputs are finite; a program needn't handle non-finite values.
Results may differ from a plain program's by a relative error of at most 0.001.
Values may be sent and summed in bfloat16 or wider, within the bound.
No kernel may reach another device: no remote copies, remote signals or barrier semaphores. Data moves between devices by JAX's collectives and lax.ppermute only.
A program may use at most 64 MiB of HBM per device.

v0:
```python
import jax
import jax.numpy as jnp
from jax import lax
from jax.sharding import Mesh
from jax.sharding import PartitionSpec as P

K = 65536
ITERS = 3
ROWS = ("rows_0", "rows_1")


TEMP = 0.07
EPS = 1e-06


def laid_out(parts, dim):
    parts = jnp.moveaxis(parts, 0, dim)
    lengths = parts.shape
    return parts.reshape(*lengths[:dim], lengths[dim] * lengths[dim + 1], *lengths[dim + 2 :])


def from_everyone(value, axis):
    copies = jnp.broadcast_to(value, (lax.axis_size(axis), *value.shape))
    return lax.all_to_all(copies, axis, split_axis=0, concat_axis=0, tiled=True)


def gathered_copies(value, axis, dim):
    return laid_out(from_everyone(value, axis), dim)


def all_blocks(value, axes, sequence):
    parts = value
    for k in sequence:
        parts = lax.all_gather(parts, axes[k])
    done = sequence[::-1]
    back = [done.index(k) for k in range(len(axes))]
    parts = parts.transpose(*back, *range(len(axes), parts.ndim))
    return parts.reshape(-1, *value.shape)


def gather_axes(value, axes, sequence, dim):
    return laid_out(all_blocks(value, axes, sequence), dim)


def by_axis(value, axes):
    for axis in axes:
        value = lax.psum(value, axis)
    return value


def taken_together(value, axis):
    everything = from_everyone(value, axis)
    return jnp.sum(everything, axis=0)


def on_device(features, prototypes, masked_index):
    chosen = jnp.take(features, masked_index, axis=0)
    patches = gathered_copies(chosen, "protos", 1)
    feat_scale = lax.rsqrt(jnp.sum(jnp.square(patches.astype(jnp.float32)), axis=1) + EPS)
    full = gather_axes(prototypes, ROWS, (0, 1), 1)
    proto_sq = jnp.sum(jnp.square(full.astype(jnp.float32)), axis=1)
    raw = lax.dot_general(
        patches, full, (((1,), (1,)), ((), ())), preferred_element_type=jnp.float32
    )
    proto_scale = lax.rsqrt(proto_sq + EPS)
    weights = jnp.exp(raw * feat_scale[:, None] * proto_scale[None, :] / TEMP)
    total_rows = masked_index.shape[0] * lax.axis_size(ROWS)
    row_scale = jnp.ones((patches.shape[0],), jnp.float32)
    for step in range(ITERS):
        col_part = jnp.dot(row_scale, weights, precision=lax.Precision.HIGHEST)
        col_scale = 1.0 / (K * by_axis(col_part, ROWS))
        row_part = jnp.dot(weights, col_scale, precision=lax.Precision.HIGHEST)
        row_scale = 1.0 / (total_rows * taken_together(row_part, "protos"))
    factor = float(K) * float(total_rows)
    return (factor * row_scale[:, None] * weights * col_scale[None, :]).astype(jnp.bfloat16)


def solution(mesh):
    split = Mesh(mesh.devices.reshape(8, 16, mesh.shape["protos"]), ("rows_0", "rows_1", "protos"))
    in_specs = (P(ROWS, "protos"), P("protos", ROWS), P(ROWS))
    out_specs = P(ROWS, "protos")
    return jax.shard_map(
        on_device, mesh=split, in_specs=in_specs, out_specs=out_specs, check_vma=False
    )
```

profile of v0, /device:TPU:1, one launch (start us, length us, event | category | flops | bytes accessed | tf_op | source)
XLA Modules:
  0.0 466.5 jit_solution(4156114515957545243)
XLA Ops:
  6.5 21.2 %all-gather = bf16[65536,2]{0,1:T(2,128)(2,1)S(1)} all-gather(bf16[8192,2]{0,1:T(2,128)(2,1)} %param.4), channel_id=2, replica_groups=mesh['rows_0'=8,'rows_1'=16,'protos'=8] {'rows_0'}, dimensions={0}, use_global_device_ids=true | all-gather | bytes 294912 | tf_op jit(solution)/shard_map/all_gather | solution.py:34
  31.9 25.5 %all_to_all.23 = bf16[8,192,32]{1,2,0:T(8,128)(2,1)S(1)} all-to-all(bf16[8,192,32]{1,2,0:T(8,128)(2,1)S(1)} %broadcast_in_dim.31), channel_id=1, replica_groups=mesh['rows_0'=8,'rows_1'=16,'protos'=8] {'protos'}, dimensions={0} | all-to-all | bytes 196608 | tf_op jit(solution)/shard_map/all_to_all | solution.py:24
  57.4 56.9 %all-gather.4.cloned.1.call-done = bf16[128,8192,2]{1,0,2:T(8,128)(2,1)} async-done(((bf16[8,8192,2]{1,0,2:T(8,128)(2,1)}), bf16[128,8192,2]{1,0,2:T(8,128)(2,1)}) %all-gather.4.cloned.1.call-update) | async-done | bytes 4194320 | tf_op jit(solution)/shard_map/all_gather | solution.py:34
  114.3 4.5 copy.18
  120.0 6.3 %copy.19 = bf16[8192,128,2]{0,2,1:T(2,128)(2,1)} copy(bf16[8192,128,2]{0,1,2:T(8,128)(2,1)S(1)} %bitcast.43) | data formatting | bytes 8388608 | tf_op jit(solution)/shard_map/transpose | solution.py:17
  126.3 7.2 %reshape.43 = bf16[8192,256]{0,1:T(8,128)(2,1)} reshape(bf16[8192,128,2]{0,2,1:T(2,128)(2,1)} %copy.19) | data formatting | bytes 8388608 | tf_op jit(solution)/shard_map/reshape | solution.py:19
  133.5 3.9 fusion.2
  137.4 2.7 copy-done
  140.1 3.0 fusion.3
  143.1 22.4 %psum.42 = f32[8192]{0:T(1024)S(1)} all-reduce(f32[8192]{0:T(1024)S(1)} %bitcast.53), channel_id=1, replica_groups=mesh['rows_0'=8,'rows_1'=16,'protos'=8] {'rows_0'}, use_global_device_ids=true, to_apply=%region_2.3 | all-reduce | flops 8192 | bytes 65536 | tf_op jit(solution)/shard_map/psum | solution.py:47
  165.5 39.9 %psum.43 = f32[8192]{0:T(1024)S(1)} all-reduce(f32[8192]{0:T(1024)S(1)} %psum.42), channel_id=1, replica_groups=mesh['rows_0'=8,'rows_1'=16,'protos'=8] {'rows_1'}, use_global_device_ids=true, to_apply=%region_3.4 | all-reduce | flops 8192 | bytes 65536 | tf_op jit(solution)/shard_map/psum | solution.py:47
  205.4 7.0 %fusion.6 = f32[1,192]{1,0:T(1,128)S(1)} fusion(f32[192,8192]{1,0:T(8,128)} %copy-done, f32[8192,1]{0,1:T(1,128)S(1)} %bitcast.49), kind=kOutput, calls=%fused_computation.24 | convolution fusion | flops 18874368 | bytes 6324992 | tf_op jit(solution)/shard_map/dot_general | solution.py:72
  212.4 40.3 %all_to_all.24 = f32[8,1,192]{2,1,0:T(1,128)S(1)} all-to-all(f32[8,1,192]{2,1,0:T(1,128)S(1)} %broadcast_in_dim.32), channel_id=1, replica_groups=mesh['rows_0'=8,'rows_1'=16,'protos'=8] {'protos'}, dimensions={0} | all-to-all | bytes 12288 | tf_op jit(solution)/shard_map/all_to_all | solution.py:24
  252.8 5.8 %fusion.7 = f32[1,8192]{1,0:T(1,128)S(1)} fusion(f32[192,1]{0,1:T(1,128)S(1)} %bitcast.57, f32[192,8192]{1,0:T(8,128)} %copy-done), kind=kOutput, calls=%fused_computation.25 | convolution fusion | flops 18874368 | bytes 6324992 | tf_op jit(solution)/shard_map/dot_general | solution.py:70
  258.6 20.4 %psum.44 = f32[8192]{0:T(1024)S(1)} all-reduce(f32[8192]{0:T(1024)S(1)} %bitcast.50), channel_id=1, replica_groups=mesh['rows_0'=8,'rows_1'=16,'protos'=8] {'rows_0'}, use_global_device_ids=true, to_apply=%region_5.6 | all-reduce | flops 8192 | bytes 65536 | tf_op jit(solution)/shard_map/psum | solution.py:47
  279.1 39.2 %psum.45 = f32[8192]{0:T(1024)S(1)} all-reduce(f32[8192]{0:T(1024)S(1)} %psum.44), channel_id=1, replica_groups=mesh['rows_0'=8,'rows_1'=16,'protos'=8] {'rows_1'}, use_global_device_ids=true, to_apply=%region_6.7 | all-reduce | flops 8192 | bytes 65536 | tf_op jit(solution)/shard_map/psum | solution.py:47
  318.3 7.0 %fusion.8 = f32[1,192]{1,0:T(1,128)S(1)} fusion(f32[192,8192]{1,0:T(8,128)} %copy-done, f32[8192,1]{0,1:T(1,128)S(1)} %bitcast.51), kind=kOutput, calls=%fused_computation.26 | convolution fusion | flops 18874368 | bytes 6324992 | tf_op jit(solution)/shard_map/dot_general | solution.py:72
  325.3 28.0 %all_to_all.25 = f32[8,1,192]{2,1,0:T(1,128)S(1)} all-to-all(f32[8,1,192]{2,1,0:T(1,128)S(1)} %broadcast_in_dim.33), channel_id=1, replica_groups=mesh['rows_0'=8,'rows_1'=16,'protos'=8] {'protos'}, dimensions={0} | all-to-all | bytes 12288 | tf_op jit(solution)/shard_map/all_to_all | solution.py:24
  353.3 5.8 %fusion.9 = f32[1,8192]{1,0:T(1,128)S(1)} fusion(f32[192,1]{0,1:T(1,128)S(1)} %bitcast.58, f32[192,8192]{1,0:T(8,128)} %copy-done), kind=kOutput, calls=%fused_computation.27 | convolution fusion | flops 18874368 | bytes 6324992 | tf_op jit(solution)/shard_map/dot_general | solution.py:70
  359.1 20.6 %psum.46 = f32[8192]{0:T(1024)S(1)} all-reduce(f32[8192]{0:T(1024)S(1)} %bitcast.52), channel_id=1, replica_groups=mesh['rows_0'=8,'rows_1'=16,'protos'=8] {'rows_0'}, use_global_device_ids=true, to_apply=%region_8.9 | all-reduce | flops 8192 | bytes 65536 | tf_op jit(solution)/shard_map/psum | solution.py:47
  379.8 38.8 %psum.47 = f32[8192]{0:T(1024)S(1)} all-reduce(f32[8192]{0:T(1024)S(1)} %psum.46), channel_id=1, replica_groups=mesh['rows_0'=8,'rows_1'=16,'protos'=8] {'rows_1'}, use_global_device_ids=true, to_apply=%region_9.10 | all-reduce | flops 8192 | bytes 65536 | tf_op jit(solution)/shard_map/psum | solution.py:47
  418.6 7.0 %fusion.10 = f32[1,192]{1,0:T(1,128)S(1)} fusion(f32[192,8192]{1,0:T(8,128)} %copy-done, f32[8192,1]{0,1:T(1,128)S(1)} %bitcast.48), kind=kOutput, calls=%fused_computation.28 | convolution fusion | flops 18874368 | bytes 6324992 | tf_op jit(solution)/shard_map/dot_general | solution.py:72
  425.6 28.8 %all_to_all.26 = f32[8,1,192]{2,1,0:T(1,128)S(1)} all-to-all(f32[8,1,192]{2,1,0:T(1,128)S(1)} %broadcast_in_dim.34), channel_id=1, replica_groups=mesh['rows_0'=8,'rows_1'=16,'protos'=8] {'protos'}, dimensions={0} | all-to-all | bytes 12288 | tf_op jit(solution)/shard_map/all_to_all | solution.py:24
  454.4 5.3 %multiply_convert_fusion = bf16[192,8192]{1,0:T(8,128)(2,1)} fusion(f32[192,8192]{1,0:T(8,128)} %copy-done, f32[8192]{0:T(1024)S(1)} %multiply_divide_fusion, f32[192]{0:T(256)S(1)} %divide_multiply_fusion), kind=kLoop, calls=%fused_computation.6 | loop fusion | flops 4718592 | bytes 9470720 | tf_op jit(solution)/shard_map/convert_element_type | solution.py:75
  (28 shorter events, 5.5 us)
Async XLA Ops:
  6.5 107.8 %all-gather.4.cloned.1.call-start = ((), (), s32[]{:S(2)}) async-start(), calls=%async_computation.4 | async-start | bytes 4456448 | tf_op jit(solution)/shard_map/all_gather | solution.py:34
  137.4 2.7 copy-start
Sparse Core Ops, SparseCore 0:
  28.7 85.5 all-gather.3
where the time goes:
time: 467 us
  blocking collectives  325 us (70%)
  waiting for transfers between devices  56.9 us (12%)
  matrix products  39.6 us (8%)
  local copies, waits for them, and re-layouts  23.3 us (5%)
  between operations  13.5 us (3%)
  other arithmetic  8.09 us (2%)
    psum x6, blocking collectives, by_axis(): value = lax.psum(value, axis)  181 us
    all_to_all x4, blocking collectives, from_everyone(): return lax.all_to_all(copies, axis, split_axis=0, concat_axis=0, tiled=True)  123 us
    all_gather x1, waiting for transfers between devices, all_blocks(): parts = lax.all_gather(parts, axes[k])  56.9 us
    all_gather x1, blocking collectives, all_blocks(): parts = lax.all_gather(parts, axes[k])  21.2 us
    dot_general x3, matrix products, on_device(): row_part = jnp.dot(weights, col_scale, precision=lax.Precision.HIGHEST)  20.9 us
    dot_general x3, matrix products, on_device(): col_part = jnp.dot(row_scale, weights, precision=lax.Precision.HIGHEST)  14.7 us
  transfers between devices with their start and end apart: 1, of which 1 were waited for; matrix products, arithmetic and copies ran while one was open for 1% of the time, Pallas kernels for 0%

commit v1 on v0

v1 whole, which is shorter than its diff:
```python
import jax
import jax.numpy as jnp
from jax import lax
from jax.sharding import Mesh
from jax.sharding import PartitionSpec as P

K = 65536
ITERS = 3
TEMP = 0.07
EPS = 1e-06
NY = 8


def exchange(value, axes):
    return lax.all_to_all(value, axes, split_axis=0, concat_axis=0, tiled=True)


def from_everyone(value, axes):
    copies = jnp.broadcast_to(value, (lax.axis_size(axes), *value.shape))
    return exchange(copies, axes)


def on_device(features, prototypes, masked_index):
    n = masked_index.shape[0]
    ny, nz, npr = lax.axis_size("y"), lax.axis_size("z"), lax.axis_size("p")
    total_rows = n * ny * nz
    k_out = prototypes.shape[0]
    k_own = k_out // ny
    picks = (lax.broadcasted_iota(jnp.int32, (features.shape[0], n), 0) == masked_index[None, :])
    chosen = lax.dot_general(
        features, picks.astype(jnp.bfloat16), (((0,), (0,)), ((), ())),
        preferred_element_type=jnp.float32,
    ).astype(jnp.bfloat16)
    slices = prototypes.T.reshape(2, ny, k_own).transpose(1, 0, 2)
    slices = jnp.broadcast_to(slices[:, None], (ny, nz, 2, k_own)).reshape(ny * nz, 2, k_own)
    protos = exchange(slices, ("y", "z")).reshape(-1, k_own)
    patches = from_everyone(chosen, ("y", "p")).reshape(ny, -1, n)
    every_proto = lax.all_gather(protos, "y")
    dim = patches.shape[1]

    feat_scale = lax.rsqrt(jnp.sum(jnp.square(patches.astype(jnp.float32)), axis=1) + EPS)
    proto_scale = lax.rsqrt(jnp.sum(jnp.square(protos.astype(jnp.float32)), axis=0) + EPS)
    raw = lax.dot_general(
        patches, protos, (((1,), (0,)), ((), ())), preferred_element_type=jnp.float32
    )
    weights = jnp.exp(raw * feat_scale[:, :, None] * proto_scale[None, None, :] / TEMP)

    row_scale = None
    for step in range(ITERS):
        scaled = weights if row_scale is None else weights * row_scale[:, :, None]
        col_part = jnp.sum(scaled, axis=(0, 1)).reshape(-1, 128)
        col_sum = jnp.sum(from_everyone(col_part, "z"), axis=0).reshape(k_own)
        col_scale = 1.0 / (K * col_sum)
        row_part = jnp.sum(weights * col_scale[None, None, :], axis=2)
        if step + 1 < ITERS:
            row_sum = jnp.sum(from_everyone(row_part, ("y", "p")), axis=0)
            row_scale = 1.0 / (total_rows * row_sum)
    sent = jnp.concatenate(
        [row_part, jnp.broadcast_to(col_scale[None], (ny, k_own))], axis=1)
    width = sent.shape[1]
    sent = jnp.broadcast_to(sent[:, None], (ny, npr, width)).reshape(ny * npr, width)
    got = exchange(sent, ("y", "p")).reshape(ny, npr, width)
    row_scale = 1.0 / (total_rows * jnp.sum(got[:, :, :n], axis=(0, 1)))
    me_p = lax.axis_index("p")
    me_y = lax.axis_index("y")
    col_all = lax.dynamic_index_in_dim(got, me_p, 1, keepdims=False)[:, n:]
    mine = lax.dynamic_index_in_dim(patches, me_y, 0, keepdims=False)
    mine_scale = lax.dynamic_index_in_dim(feat_scale, me_y, 0, keepdims=False)
    every_scale = lax.rsqrt(jnp.sum(jnp.square(every_proto.astype(jnp.float32)), axis=1) + EPS)
    raw_out = lax.dot_general(
        mine, every_proto, (((0,), (1,)), ((), ())), preferred_element_type=jnp.float32
    )
    w_out = jnp.exp(raw_out * mine_scale[:, None, None] * every_scale[None] / TEMP)
    factor = float(K) * float(total_rows)
    out = (factor * row_scale)[:, None, None] * w_out * col_all[None]
    return out.astype(jnp.bfloat16).reshape(n, k_out)


def solution(mesh):
    rows = mesh.shape["rows"]
    split = Mesh(mesh.devices.reshape(NY, rows // NY, mesh.shape["protos"]), ("y", "z", "p"))
    in_specs = (P(("y", "z"), "p"), P("p", ("y", "z")), P(("y", "z")))
    out_specs = P(("y", "z"), "p")
    return jax.shard_map(
        on_device, mesh=split, in_specs=in_specs, out_specs=out_specs, check_vma=False
    )
```

time: 467 us -> 268 us (0.57)
  blocking collectives: 325 us -> 101 us
  starting transfers between devices: 0.01 us -> 42.1 us
  matrix products: 39.6 us -> 8.86 us
  waiting for transfers between devices: 56.9 us -> 72.3 us
  local copies, waits for them, and re-layouts: 23.3 us -> 8.39 us
  other arithmetic: 8.09 us -> 21.1 us
    psum x6 -> x0, blocking collectives: 181 us -> none  [by_axis(): value = lax.psum(value, axis)]
    all_to_all x0 -> x3, waiting for transfers between devices: none -> 72.3 us  [exchange(): return lax.all_to_all(value, axes, split_axis=0, concat_axis=0, tiled=True)]
    all_gather x1, waiting for transfers between devices: 56.9 us -> 0.02 us  [on_device(): every_proto = lax.all_gather(protos, 'y')]
    all_to_all x0 -> x3, starting transfers between devices: none -> 42.1 us  [exchange(): return lax.all_to_all(value, axes, split_axis=0, concat_axis=0, tiled=True)]
    dot_general x7 -> x3, matrix products: 39.6 us -> 8.86 us  [the longest x1 4.4 us: on_device(): lax.dot_general(mine, every_proto, (((0,), (1,)), ((), ())), preferred_el...]
    all_to_all x4 -> x5, blocking collectives: 123 us -> 101 us  [exchange(): return lax.all_to_all(value, axes, split_axis=0, concat_axis=0, tiled=True)]
    all_gather x1 -> x0, blocking collectives: 21.2 us -> none  [all_blocks(): parts = lax.all_gather(parts, axes[k])]
    reduce_sum x4 -> x13, other arithmetic: 1.22 us -> 20.6 us  [the longest x3 9.95 us: on_device(): row_part = jnp.sum(weights * col_scale[None, None, :], axis=2)]
  transfers between devices with their start and end apart: 1 -> 4, of which waited for: 1 -> 3; matrix products, arithmetic and copies ran while one was open for 1% -> 9% of each run, Pallas kernels for 0% -> 0%
where the time goes in v1:
time: 268 us; the launch traced here: 267 us
  blocking collectives  101 us (38%)
  waiting for transfers between devices  72.3 us (27%)
  starting transfers between devices  42.1 us (16%)
  other arithmetic  21.1 us (8%)
  between operations  13.6 us (5%)
  matrix products  8.86 us (3%)
  local copies, waits for them, and re-layouts  8.39 us (3%)
    all_to_all x5, blocking collectives, exchange(): return lax.all_to_all(value, axes, split_axis=0, concat_axis=0, tiled=True)  101 us
    all_to_all x3, waiting for transfers between devices, exchange(): return lax.all_to_all(value, axes, split_axis=0, concat_axis=0, tiled=True)  72.3 us
    all_to_all x3, starting transfers between devices, exchange(): return lax.all_to_all(value, axes, split_axis=0, concat_axis=0, tiled=True)  42.1 us
    reduce_sum x3, other arithmetic, on_device(): row_part = jnp.sum(weights * col_scale[None, None, :], axis=2)  9.95 us
    reduce_sum x2, other arithmetic, on_device(): col_part = jnp.sum(scaled, axis=(0, 1)).reshape(-1, 128)  6.59 us
  transfers between devices with their start and end apart: 4, of which 3 were waited for; matrix products, arithmetic and copies ran while one was open for 9% of the time, Pallas kernels for 0%

profile of v1, /device:TPU:1, one launch (start us, length us, event | category | flops | bytes accessed | tf_op | source)
XLA Modules:
  0.0 267.0 jit_solution(17321432782408394508)
XLA Ops:
  8.1 1.1 broadcast_in_dim.18
  9.2 18.2 %all-to-all-start = ((bf16[64,32,192]{2,1,0:T(8,128)(2,1)}), bf16[64,32,192]{2,1,0:T(8,128)(2,1)S(1)}, u32[]{:S(2)}, u32[]{:S(2)}) async-start(bf16[64,32,192]{2,1,0:T(8,128)(2,1)} %broadcast_in_dim.18), calls=%async_computation | async-start | bytes 2097152 | tf_op jit(solution)/shard_map/all_to_all | solution.py:15
  28.3 27.5 %all-to-all-done = bf16[64,32,192]{2,1,0:T(8,128)(2,1)S(1)} async-done(((bf16[64,32,192]{2,1,0:T(8,128)(2,1)}), bf16[64,32,192]{2,1,0:T(8,128)(2,1)S(1)}, u32[]{:S(2)}, u32[]{:S(2)}) %all-to-all-start) | async-done | bytes 786464 | tf_op jit(solution)/shard_map/all_to_all | solution.py:15
  55.8 1.1 broadcast_in_dim.19
  56.8 16.5 %all-to-all-start.1 = ((bf16[128,2,1024]{2,1,0:T(2,128)(2,1)}), bf16[128,2,1024]{2,1,0:T(2,128)(2,1)S(1)}, u32[]{:S(2)}, u32[]{:S(2)}) async-start(bf16[128,2,1024]{2,1,0:T(2,128)(2,1)} %bitcast.4), calls=%async_computation.1 | async-start | bytes 1048576 | tf_op jit(solution)/shard_map/all_to_all | solution.py:15
  73.9 30.6 %all-to-all-done.1 = bf16[128,2,1024]{2,1,0:T(2,128)(2,1)S(1)} async-done(((bf16[128,2,1024]{2,1,0:T(2,128)(2,1)}), bf16[128,2,1024]{2,1,0:T(2,128)(2,1)S(1)}, u32[]{:S(2)}, u32[]{:S(2)}) %all-to-all-start.1) | async-done | bytes 524320 | tf_op jit(solution)/shard_map/all_to_all | solution.py:15
  104.5 1.0 all_gather_reshape.3
  106.3 3.6 %fusion.6 = (f32[1024]{0:T(1024)S(1)}, f32[8,192,1024]{2,1,0:T(8,128)}) fusion(f32[1024]{0:T(1024)S(1)} %add_rsqrt_fusion.2, f32[8,192]{1,0:T(8,128)S(1)} %add_rsqrt_fusion.1, bf16[8,256,192]{2,1,0:T(8,128)(2,1)S(1)} %bitcast.42, bf16[256,1024,1]{1,0,2:T(8,128)(2,1)S(1)} %reshape.112), kind=kOutput, calls=%fused_computation.35 | convolution fusion | flops 811596800 | bytes 7616512 | tf_op jit(solution)/shard_map/dot_general | solution.py:43
  109.9 18.1 %all_to_all.44 = f32[16,8,128]{2,1,0:T(8,128)S(1)} all-to-all(f32[16,8,128]{2,1,0:T(8,128)S(1)} %broadcast_in_dim.20), channel_id=1, replica_groups=mesh['y'=8,'z'=16,'p'=8] {'z'}, dimensions={0} | all-to-all | bytes 131072 | tf_op jit(solution)/shard_map/all_to_all | solution.py:15
  128.1 3.4 %multiply_reduce_fusion.5 = f32[8,192]{1,0:T(8,128)S(1)} fusion(f32[8,192,1024]{2,1,0:T(8,128)} %get-tuple-element.6, f32[1024]{0:T(1024)S(1)} %divide_bitcast_fusion.2), kind=kLoop, calls=%fused_computation.6 | loop fusion | flops 3144192 | bytes 6301696 | tf_op jit(solution)/shard_map/reduce_sum | solution.py:54
  131.5 29.5 %all_to_all.45 = f32[64,8,192]{2,1,0:T(8,128)S(1)} all-to-all(f32[64,8,192]{2,1,0:T(8,128)S(1)} %broadcast_in_dim.21), channel_id=1, replica_groups=mesh['y'=8,'z'=16,'p'=8] {'y','p'}, dimensions={0} | all-to-all | bytes 786432 | tf_op jit(solution)/shard_map/all_to_all | solution.py:15
  161.1 3.3 %multiply_reduce_fusion.4 = f32[1024]{0:T(1024)S(1)} fusion(f32[8,192,1024]{2,1,0:T(8,128)} %get-tuple-element.6, f32[8,192]{1,0:T(8,128)S(1)} %multiply_divide_fusion.1), kind=kLoop, calls=%fused_computation.5 | loop fusion | flops 3144704 | bytes 6301696 | tf_op jit(solution)/shard_map/reduce_sum | solution.py:51
  164.4 14.2 %all_to_all.46 = f32[16,8,128]{2,1,0:T(8,128)S(1)} all-to-all(f32[16,8,128]{2,1,0:T(8,128)S(1)} %broadcast_in_dim.22), channel_id=1, replica_groups=mesh['y'=8,'z'=16,'p'=8] {'z'}, dimensions={0} | all-to-all | bytes 131072 | tf_op jit(solution)/shard_map/all_to_all | solution.py:15
  178.7 3.3 %multiply_reduce_fusion.3 = f32[8,192]{1,0:T(8,128)S(1)} fusion(f32[8,192,1024]{2,1,0:T(8,128)} %get-tuple-element.6, f32[1024]{0:T(1024)S(1)} %divide_bitcast_fusion.1), kind=kLoop, calls=%fused_computation.4 | loop fusion | flops 3144192 | bytes 6301696 | tf_op jit(solution)/shard_map/reduce_sum | solution.py:54
  182.0 24.5 %all_to_all.47 = f32[64,8,192]{2,1,0:T(8,128)S(1)} all-to-all(f32[64,8,192]{2,1,0:T(8,128)S(1)} %broadcast_in_dim.23), channel_id=1, replica_groups=mesh['y'=8,'z'=16,'p'=8] {'y','p'}, dimensions={0} | all-to-all | bytes 786432 | tf_op jit(solution)/shard_map/all_to_all | solution.py:15
  206.6 3.3 %multiply_reduce_fusion.2 = f32[1024]{0:T(1024)S(1)} fusion(f32[8,192,1024]{2,1,0:T(8,128)} %get-tuple-element.6, f32[8,192]{1,0:T(8,128)S(1)} %multiply_divide_fusion), kind=kLoop, calls=%fused_computation.3 | loop fusion | flops 3144704 | bytes 6301696 | tf_op jit(solution)/shard_map/reduce_sum | solution.py:51
  209.9 14.3 %all_to_all.48 = f32[16,8,128]{2,1,0:T(8,128)S(1)} all-to-all(f32[16,8,128]{2,1,0:T(8,128)S(1)} %broadcast_in_dim.24), channel_id=1, replica_groups=mesh['y'=8,'z'=16,'p'=8] {'z'}, dimensions={0} | all-to-all | bytes 131072 | tf_op jit(solution)/shard_map/all_to_all | solution.py:15
  224.3 3.3 %multiply_reduce_fusion.1 = f32[8,192]{1,0:T(8,128)S(1)} fusion(f32[8,192,1024]{2,1,0:T(8,128)} %get-tuple-element.6, f32[1024]{0:T(1024)S(1)} %divide_bitcast_fusion), kind=kLoop, calls=%fused_computation.2 | loop fusion | flops 3144192 | bytes 6301696 | tf_op jit(solution)/shard_map/reduce_sum | solution.py:54
  227.6 1.1 all_to_all.34
  228.7 7.3 %all-to-all-start.7 = ((f32[64,1,1216]{2,1,0:T(1,128)}), f32[64,1,1216]{2,1,0:T(1,128)S(1)}, u32[]{:S(2)}, u32[]{:S(2)}) async-start(f32[64,1,1216]{2,1,0:T(1,128)} %all_to_all.34), calls=%async_computation.7 | async-start | bytes 655360 | tf_op jit(solution)/shard_map/all_to_all | solution.py:15
  236.0 14.2 %all-to-all-done.7 = f32[64,1,1216]{2,1,0:T(1,128)S(1)} async-done(((f32[64,1,1216]{2,1,0:T(1,128)}), f32[64,1,1216]{2,1,0:T(1,128)S(1)}, u32[]{:S(2)}, u32[]{:S(2)}) %all-to-all-start.7) | async-done | bytes 311328 | tf_op jit(solution)/shard_map/all_to_all | solution.py:15
  250.4 3.2 %multiply_reduce_fusion = f32[8,1024]{1,0:T(8,128)S(1)} fusion(bf16[8,256,1024]{2,1,0:T(8,128)(2,1)} %all-gather.2.cloned.1.call-done), kind=kLoop, calls=%fused_computation | loop fusion | flops 6283264 | bytes 4227072 | tf_op jit(solution)/shard_map/reduce_sum | solution.py:69
  253.6 4.4 %fusion = bf16[8,24,8,1024]{3,2,1,0:T(8,128)(2,1)S(1)} fusion(f32[8,1024]{1,0:T(8,128)S(1)} %slice.9, f32[8,1024]{1,0:T(8,128)S(1)} %add_rsqrt_fusion, f32[192]{0:T(256)S(1)} %bitcast.52, f32[192]{0:T(256)S(1)} %divide_multiply_fusion, bf16[8,256,1024]{2,1,0:T(8,128)(2,1)} %all-gather.2.cloned.1.call-done, bf16[8,256,192]{2,1,0:T(8,128)(2,1)S(1)} %bitcast.43, ...), kind=kOutput, calls=%fused_computation.8 | convolution fusion | flops 814743552 | bytes 7538692 | tf_op jit(solution)/shard_map/dot_general | solution.py:70
  258.0 2.1 copy.20
  (40 shorter events, 4.4 us)
Async XLA Ops:
  6.5 0.7 copy-start
  9.2 46.5 %all-to-all-start = ((bf16[64,32,192]{2,1,0:T(8,128)(2,1)}), bf16[64,32,192]{2,1,0:T(8,128)(2,1)S(1)}, u32[]{:S(2)}, u32[]{:S(2)}) async-start(bf16[64,32,192]{2,1,0:T(8,128)(2,1)} %broadcast_in_dim.18), calls=%async_computation | async-start | bytes 2097152 | tf_op jit(solution)/shard_map/all_to_all | solution.py:15
  56.8 47.7 %all-to-all-start.1 = ((bf16[128,2,1024]{2,1,0:T(2,128)(2,1)}), bf16[128,2,1024]{2,1,0:T(2,128)(2,1)S(1)}, u32[]{:S(2)}, u32[]{:S(2)}) async-start(bf16[128,2,1024]{2,1,0:T(2,128)(2,1)} %bitcast.4), calls=%async_computation.1 | async-start | bytes 1048576 | tf_op jit(solution)/shard_map/all_to_all | solution.py:15
  73.4 177.1 %all-gather.2.cloned.1.call-start = ((), (), s32[]{:S(2)}) async-start(), calls=%async_computation.8 | async-start | bytes 4718592 | tf_op jit(solution)/shard_map/all_gather | solution.py:38
  228.7 21.6 %all-to-all-start.7 = ((f32[64,1,1216]{2,1,0:T(1,128)}), f32[64,1,1216]{2,1,0:T(1,128)S(1)}, u32[]{:S(2)}, u32[]{:S(2)}) async-start(f32[64,1,1216]{2,1,0:T(1,128)} %all_to_all.34), calls=%async_computation.7 | async-start | bytes 655360 | tf_op jit(solution)/shard_map/all_to_all | solution.py:15
Sparse Core Ops, SparseCore 0:
  105.6 63.1 all-gather.1

commit v2 on v1

--- a/solution.py
+++ b/solution.py
@@ -22,19 +22,29 @@
 
 def on_device(features, prototypes, masked_index):
     n = masked_index.shape[0]
-    ny, nz, npr = lax.axis_size("y"), lax.axis_size("z"), lax.axis_size("p")
+    ny, nz = lax.axis_size("y"), lax.axis_size("z")
     total_rows = n * ny * nz
     k_out = prototypes.shape[0]
     k_own = k_out // ny
-    picks = (lax.broadcasted_iota(jnp.int32, (features.shape[0], n), 0) == masked_index[None, :])
+    lanes = -(-n // 128) * 128
+    dim = features.shape[1] * lax.axis_size("p")
+    picks = lax.broadcasted_iota(jnp.int32, (features.shape[0], lanes), 0) == jnp.pad(
+        masked_index, (0, lanes - n), constant_values=-1)[None, :]
     chosen = lax.dot_general(
         features, picks.astype(jnp.bfloat16), (((0,), (0,)), ((), ())),
         preferred_element_type=jnp.float32,
     ).astype(jnp.bfloat16)
-    slices = prototypes.T.reshape(2, ny, k_own).transpose(1, 0, 2)
-    slices = jnp.broadcast_to(slices[:, None], (ny, nz, 2, k_own)).reshape(ny * nz, 2, k_own)
-    protos = exchange(slices, ("y", "z")).reshape(-1, k_own)
-    patches = from_everyone(chosen, ("y", "p")).reshape(ny, -1, n)
+    slices = prototypes.T.reshape(2, ny, k_own // lanes, lanes).transpose(1, 0, 2, 3)
+    slices = slices.reshape(ny, -1, lanes)
+    held = slices.shape[1]
+    both = jnp.concatenate(
+        [slices, jnp.broadcast_to(chosen[None], (ny, *chosen.shape))], axis=1)
+    both = exchange(both, "y")
+    patches = lax.all_gather(both[:, held:], "p")
+    protos = both[:, :held].reshape(2 * ny, k_own)
+    protos = from_everyone(protos, "z").reshape(nz, ny, 2, k_own)
+    protos = protos.transpose(1, 0, 2, 3).reshape(dim, k_own)
+    patches = patches.transpose(1, 0, 2, 3).reshape(ny, dim, lanes)[:, :, :n]
     every_proto = lax.all_gather(protos, "y")
     dim = patches.shape[1]
 
@@ -52,18 +62,16 @@
         col_sum = jnp.sum(from_everyone(col_part, "z"), axis=0).reshape(k_own)
         col_scale = 1.0 / (K * col_sum)
         row_part = jnp.sum(weights * col_scale[None, None, :], axis=2)
+        row_part = jnp.sum(from_everyone(row_part, "p"), axis=0)
         if step + 1 < ITERS:
-            row_sum = jnp.sum(from_everyone(row_part, ("y", "p")), axis=0)
+            row_sum = jnp.sum(from_everyone(row_part, "y"), axis=0)
             row_scale = 1.0 / (total_rows * row_sum)
     sent = jnp.concatenate(
         [row_part, jnp.broadcast_to(col_scale[None], (ny, k_own))], axis=1)
-    width = sent.shape[1]
-    sent = jnp.broadcast_to(sent[:, None], (ny, npr, width)).reshape(ny * npr, width)
-    got = exchange(sent, ("y", "p")).reshape(ny, npr, width)
-    row_scale = 1.0 / (total_rows * jnp.sum(got[:, :, :n], axis=(0, 1)))
-    me_p = lax.axis_index("p")
+    got = exchange(sent, "y")
+    row_scale = 1.0 / (total_rows * jnp.sum(got[:, :n], axis=0))
+    col_all = got[:, n:]
     me_y = lax.axis_index("y")
-    col_all = lax.dynamic_index_in_dim(got, me_p, 1, keepdims=False)[:, n:]
     mine = lax.dynamic_index_in_dim(patches, me_y, 0, keepdims=False)
     mine_scale = lax.dynamic_index_in_dim(feat_scale, me_y, 0, keepdims=False)
     every_scale = lax.rsqrt(jnp.sum(jnp.square(every_proto.astype(jnp.float32)), axis=1) + EPS)

time: 268 us -> 240 us (0.90)
  waiting for transfers between devices: 72.3 us -> 44.7 us
  starting transfers between devices: 42.1 us -> 28.3 us
  blocking collectives: 101 us -> 113 us
    all_to_all x3, waiting for transfers between devices: 72.3 us -> 32.6 us  [exchange(): return lax.all_to_all(value, axes, split_axis=0, concat_axis=0, tiled=True)]
    all_to_all x3, starting transfers between devices: 42.1 us -> 28.2 us  [exchange(): return lax.all_to_all(value, axes, split_axis=0, concat_axis=0, tiled=True)]
    all_to_all x5 -> x8, blocking collectives: 101 us -> 113 us  [exchange(): return lax.all_to_all(value, axes, split_axis=0, concat_axis=0, tiled=True)]
    all_gather x0 -> x1, waiting for transfers between devices: none -> 12.1 us  [on_device(): patches = lax.all_gather(both[:, held:], 'p')]
  transfers between devices with their start and end apart: 4 -> 5, of which waited for: 3 -> 4; matrix products, arithmetic and copies ran while one was open for 9% -> 11% of each run, Pallas kernels for 0% -> 0%
where the time goes in v2:
time: 240 us; the launch traced here: 239 us
  blocking collectives  113 us (47%)
  waiting for transfers between devices  44.7 us (19%)
  starting transfers between devices  28.3 us (12%)
  other arithmetic  20.4 us (8%)
  between operations  13.6 us (6%)
  local copies, waits for them, and re-layouts  10.5 us (4%)
  matrix products  8.18 us (3%)
    all_to_all x8, blocking collectives, exchange(): return lax.all_to_all(value, axes, split_axis=0, concat_axis=0, tiled=True)  113 us
    all_to_all x3, waiting for transfers between devices, exchange(): return lax.all_to_all(value, axes, split_axis=0, concat_axis=0, tiled=True)  32.6 us
    all_to_all x3, starting transfers between devices, exchange(): return lax.all_to_all(value, axes, split_axis=0, concat_axis=0, tiled=True)  28.2 us
    all_gather x1, waiting for transfers between devices, on_device(): patches = lax.all_gather(both[:, held:], 'p')  12.1 us
    reduce_sum x3, other arithmetic, on_device(): row_part = jnp.sum(weights * col_scale[None, None, :], axis=2)  9.92 us
    reduce_sum x2, other arithmetic, on_device(): col_part = jnp.sum(scaled, axis=(0, 1)).reshape(-1, 128)  6.59 us
  transfers between devices with their start and end apart: 5, of which 4 were waited for; matrix products, arithmetic and copies ran while one was open for 11% of the time, Pallas kernels for 0%

profile of v2, /device:TPU:1, one launch (start us, length us, event | category | flops | bytes accessed | tf_op | source)
XLA Modules:
  0.0 238.5 jit_solution(9152533633803972149)
XLA Ops:
  8.3 15.7 %all_to_all.62 = bf16[8,40,256]{2,1,0:T(8,128)(2,1)S(1)} all-to-all(bf16[8,40,256]{2,1,0:T(8,128)(2,1)S(1)} %pad_maximum_fusion), channel_id=1, replica_groups=mesh['y'=8,'z'=16,'p'=8] {'y'}, dimensions={0} | all-to-all | bytes 327680 | tf_op jit(solution)/shard_map/all_to_all | solution.py:15
  24.9 18.5 %all-to-all-start.1 = ((bf16[16,16,1024]{2,1,0:T(8,128)(2,1)}), bf16[16,16,1024]{2,1,0:T(8,128)(2,1)S(1)}, u32[]{:S(2)}, u32[]{:S(2)}) async-start(bf16[16,16,1024]{2,1,0:T(8,128)(2,1)} %broadcast_in_dim.23), calls=%async_computation.1 | async-start | bytes 1048576 | tf_op jit(solution)/shard_map/all_to_all | solution.py:15
  44.2 20.9 %all-to-all-done.1 = bf16[16,16,1024]{2,1,0:T(8,128)(2,1)S(1)} async-done(((bf16[16,16,1024]{2,1,0:T(8,128)(2,1)}), bf16[16,16,1024]{2,1,0:T(8,128)(2,1)S(1)}, u32[]{:S(2)}, u32[]{:S(2)}) %all-to-all-start.1) | async-done | bytes 524320 | tf_op jit(solution)/shard_map/all_to_all | solution.py:15
  67.0 12.1 %all-gather.6.cloned.1.call-done = bf16[64,32,256]{2,1,0:T(8,128)(2,1)} async-done(((bf16[8,32,256]{2,1,0:T(8,128)(2,1)}), bf16[64,32,256]{2,1,0:T(8,128)(2,1)}) %all-gather.6.cloned.1.call-update) | async-done | bytes 1048592 | tf_op jit(solution)/shard_map/all_gather | solution.py:43
  81.6 3.6 %fusion.7 = (f32[1024]{0:T(1024)S(1)}, f32[8,192,1024]{2,1,0:T(8,128)}) fusion(f32[1024]{0:T(1024)S(1)} %add_rsqrt_fusion.2, f32[8,192]{1,0:T(8,128)S(1)} %add_rsqrt_fusion.1, bf16[256,1024,1]{1,0,2:T(8,128)(2,1)S(1)} %reshape.112, bf16[8,256,256]{2,1,0:T(8,128)(2,1)S(1)} %bitcast.39), kind=kOutput, calls=%fused_computation.33 | convolution fusion | flops 811596800 | bytes 7878656 | tf_op jit(solution)/shard_map/dot_general | solution.py:53
  85.2 24.1 %all_to_all.63 = f32[16,8,128]{2,1,0:T(8,128)S(1)} all-to-all(f32[16,8,128]{2,1,0:T(8,128)S(1)} %broadcast_in_dim.24), channel_id=1, replica_groups=mesh['y'=8,'z'=16,'p'=8] {'z'}, dimensions={0} | all-to-all | bytes 131072 | tf_op jit(solution)/shard_map/all_to_all | solution.py:15
  109.4 3.3 %multiply_reduce_fusion.5 = f32[8,192]{1,0:T(8,128)S(1)} fusion(f32[8,192,1024]{2,1,0:T(8,128)} %get-tuple-element.6, f32[1024]{0:T(1024)S(1)} %divide_bitcast_fusion.2), kind=kLoop, calls=%fused_computation.6 | loop fusion | flops 3144192 | bytes 6301696 | tf_op jit(solution)/shard_map/reduce_sum | solution.py:64
  112.7 9.7 %all_to_all.64 = f32[8,8,192]{2,1,0:T(8,128)S(1)} all-to-all(f32[8,8,192]{2,1,0:T(8,128)S(1)} %broadcast_in_dim.25), channel_id=1, replica_groups=mesh['y'=8,'z'=16,'p'=8] {'p'}, dimensions={0} | all-to-all | bytes 98304 | tf_op jit(solution)/shard_map/all_to_all | solution.py:15
  122.5 14.4 %all_to_all.65 = f32[8,8,192]{2,1,0:T(8,128)S(1)} all-to-all(f32[8,8,192]{2,1,0:T(8,128)S(1)} %broadcast_in_dim.26), channel_id=1, replica_groups=mesh['y'=8,'z'=16,'p'=8] {'y'}, dimensions={0} | all-to-all | bytes 98304 | tf_op jit(solution)/shard_map/all_to_all | solution.py:15
  136.9 3.3 %multiply_reduce_fusion.4 = f32[1024]{0:T(1024)S(1)} fusion(f32[8,192,1024]{2,1,0:T(8,128)} %get-tuple-element.6, f32[8,192]{1,0:T(8,128)S(1)} %multiply_divide_fusion.1), kind=kLoop, calls=%fused_computation.5 | loop fusion | flops 3144704 | bytes 6301696 | tf_op jit(solution)/shard_map/reduce_sum | solution.py:61
  140.2 14.2 %all_to_all.66 = f32[16,8,128]{2,1,0:T(8,128)S(1)} all-to-all(f32[16,8,128]{2,1,0:T(8,128)S(1)} %broadcast_in_dim.27), channel_id=1, replica_groups=mesh['y'=8,'z'=16,'p'=8] {'z'}, dimensions={0} | all-to-all | bytes 131072 | tf_op jit(solution)/shard_map/all_to_all | solution.py:15
  154.4 3.3 %multiply_reduce_fusion.3 = f32[8,192]{1,0:T(8,128)S(1)} fusion(f32[8,192,1024]{2,1,0:T(8,128)} %get-tuple-element.6, f32[1024]{0:T(1024)S(1)} %divide_bitcast_fusion.1), kind=kLoop, calls=%fused_computation.4 | loop fusion | flops 3144192 | bytes 6301696 | tf_op jit(solution)/shard_map/reduce_sum | solution.py:64
  157.7 10.8 %all_to_all.67 = f32[8,8,192]{2,1,0:T(8,128)S(1)} all-to-all(f32[8,8,192]{2,1,0:T(8,128)S(1)} %broadcast_in_dim.28), channel_id=1, replica_groups=mesh['y'=8,'z'=16,'p'=8] {'p'}, dimensions={0} | all-to-all | bytes 98304 | tf_op jit(solution)/shard_map/all_to_all | solution.py:15
  168.5 9.7 %all_to_all.68 = f32[8,8,192]{2,1,0:T(8,128)S(1)} all-to-all(f32[8,8,192]{2,1,0:T(8,128)S(1)} %broadcast_in_dim.58), channel_id=1, replica_groups=mesh['y'=8,'z'=16,'p'=8] {'y'}, dimensions={0} | all-to-all | bytes 98304 | tf_op jit(solution)/shard_map/all_to_all | solution.py:15
  178.2 3.3 %multiply_reduce_fusion.2 = f32[1024]{0:T(1024)S(1)} fusion(f32[8,192,1024]{2,1,0:T(8,128)} %get-tuple-element.6, f32[8,192]{1,0:T(8,128)S(1)} %multiply_divide_fusion), kind=kLoop, calls=%fused_computation.3 | loop fusion | flops 3144704 | bytes 6301696 | tf_op jit(solution)/shard_map/reduce_sum | solution.py:61
  181.5 14.2 %all_to_all.69 = f32[16,8,128]{2,1,0:T(8,128)S(1)} all-to-all(f32[16,8,128]{2,1,0:T(8,128)S(1)} %broadcast_in_dim.59), channel_id=1, replica_groups=mesh['y'=8,'z'=16,'p'=8] {'z'}, dimensions={0} | all-to-all | bytes 131072 | tf_op jit(solution)/shard_map/all_to_all | solution.py:15
  195.8 3.3 %multiply_reduce_fusion.1 = f32[8,192]{1,0:T(8,128)S(1)} fusion(f32[8,192,1024]{2,1,0:T(8,128)} %get-tuple-element.6, f32[1024]{0:T(1024)S(1)} %divide_bitcast_fusion), kind=kLoop, calls=%fused_computation.2 | loop fusion | flops 3144192 | bytes 6301696 | tf_op jit(solution)/shard_map/reduce_sum | solution.py:64
  199.7 6.4 %all-to-all-start.9 = ((f32[8,8,192]{2,1,0:T(8,128)}), f32[8,8,192]{2,1,0:T(8,128)S(1)}, u32[]{:S(2)}, u32[]{:S(2)}) async-start(f32[8,8,192]{2,1,0:T(8,128)} %broadcast_in_dim.60), calls=%async_computation.9 | async-start | bytes 131072 | tf_op jit(solution)/shard_map/all_to_all | solution.py:15
  206.2 4.8 %all-to-all-done.9 = f32[8,8,192]{2,1,0:T(8,128)S(1)} async-done(((f32[8,8,192]{2,1,0:T(8,128)}), f32[8,8,192]{2,1,0:T(8,128)S(1)}, u32[]{:S(2)}, u32[]{:S(2)}) %all-to-all-start.9) | async-done | bytes 49184 | tf_op jit(solution)/shard_map/all_to_all | solution.py:15
  211.6 3.3 %all-to-all-start.10 = ((f32[8,1,1216]{2,1,0:T(1,128)}), f32[8,1,1216]{2,1,0:T(1,128)S(1)}, u32[]{:S(2)}, u32[]{:S(2)}) async-start(f32[8,1,1216]{2,1,0:T(1,128)} %all_to_all.48), calls=%async_computation.10 | async-start | bytes 81920 | tf_op jit(solution)/shard_map/all_to_all | solution.py:15
  215.0 6.9 %all-to-all-done.10 = f32[8,1,1216]{2,1,0:T(1,128)S(1)} async-done(((f32[8,1,1216]{2,1,0:T(1,128)}), f32[8,1,1216]{2,1,0:T(1,128)S(1)}, u32[]{:S(2)}, u32[]{:S(2)}) %all-to-all-start.10) | async-done | bytes 38944 | tf_op jit(solution)/shard_map/all_to_all | solution.py:15
  222.0 3.2 %multiply_reduce_fusion = f32[8,1024]{1,0:T(8,128)S(1)} fusion(bf16[8,256,1024]{2,1,0:T(8,128)(2,1)} %all-gather.4.cloned.1.call-done), kind=kLoop, calls=%fused_computation | loop fusion | flops 6283264 | bytes 4227072 | tf_op jit(solution)/shard_map/reduce_sum | solution.py:77
  225.2 4.4 %fusion = bf16[8,24,8,1024]{3,2,1,0:T(8,128)(2,1)S(1)} fusion(f32[8,1024]{1,0:T(8,128)S(1)} %slice.24, f32[8,1024]{1,0:T(8,128)S(1)} %add_rsqrt_fusion, f32[192]{0:T(256)S(1)} %bitcast.49, f32[192]{0:T(256)S(1)} %divide_multiply_fusion, bf16[8,256,1024]{2,1,0:T(8,128)(2,1)} %all-gather.4.cloned.1.call-done, bf16[8,256,192]{1,2,0:T(8,128)(2,1)S(1)} %copy.41, ...), kind=kOutput, calls=%fused_computation.8 | convolution fusion | flops 814743552 | bytes 7505924 | tf_op jit(solution)/shard_map/dot_general | solution.py:78
  229.6 2.1 copy.42
  (58 shorter events, 9.4 us)
Async XLA Ops:
  6.5 1.5 copy-start
  24.9 40.2 %all-to-all-start.1 = ((bf16[16,16,1024]{2,1,0:T(8,128)(2,1)}), bf16[16,16,1024]{2,1,0:T(8,128)(2,1)S(1)}, u32[]{:S(2)}, u32[]{:S(2)}) async-start(bf16[16,16,1024]{2,1,0:T(8,128)(2,1)} %broadcast_in_dim.23), calls=%async_computation.1 | async-start | bytes 1048576 | tf_op jit(solution)/shard_map/all_to_all | solution.py:15
  43.4 35.6 %all-gather.6.cloned.1.call-start = ((), (), s32[]{:S(2)}) async-start(), calls=%async_computation.12 | async-start | bytes 1179648 | tf_op jit(solution)/shard_map/all_gather | solution.py:43
  44.2 177.8 %all-gather.4.cloned.1.call-start = ((), (), s32[]{:S(2)}) async-start(), calls=%async_computation.11 | async-start | bytes 4718592 | tf_op jit(solution)/shard_map/all_gather | solution.py:48
  199.7 11.2 %all-to-all-start.9 = ((f32[8,8,192]{2,1,0:T(8,128)}), f32[8,8,192]{2,1,0:T(8,128)S(1)}, u32[]{:S(2)}, u32[]{:S(2)}) async-start(f32[8,8,192]{2,1,0:T(8,128)} %broadcast_in_dim.60), calls=%async_computation.9 | async-start | bytes 131072 | tf_op jit(solution)/shard_map/all_to_all | solution.py:15
  211.6 10.2 %all-to-all-start.10 = ((f32[8,1,1216]{2,1,0:T(1,128)}), f32[8,1,1216]{2,1,0:T(1,128)S(1)}, u32[]{:S(2)}, u32[]{:S(2)}) async-start(f32[8,1,1216]{2,1,0:T(1,128)} %all_to_all.48), calls=%async_computation.10 | async-start | bytes 81920 | tf_op jit(solution)/shard_map/all_to_all | solution.py:15
Sparse Core Ops, SparseCore 0:
  47.0 32.0 all-gather.5
  81.7 63.3 all-gather.3

commit v3 on v2

v3 whole, which is shorter than its diff:
```python
import functools

import jax
import jax.numpy as jnp
from jax import lax
from jax.experimental import pallas as pl
from jax.experimental.pallas import tpu as pltpu
from jax.sharding import Mesh
from jax.sharding import PartitionSpec as P


K = 65536
ITERS = 3
TEMP = 0.07
EPS = 1e-06
NY = 8
LANES = 128
VMEM = pl.BlockSpec(memory_space=pltpu.VMEM)
HIGHEST = lax.Precision.HIGHEST


def exchange(value, axes):
    return lax.all_to_all(value, axes, split_axis=0, concat_axis=0, tiled=True)


def from_everyone(value, axes):
    copies = jnp.broadcast_to(value, (lax.axis_size(axes), *value.shape))
    return exchange(copies, axes)


def call(body, out_shape, flops, moved, limit=20 * 2**20, **kwargs):
    return pl.pallas_call(
        body,
        out_shape=out_shape,
        cost_estimate=pl.CostEstimate(flops=flops, bytes_accessed=moved, transcendentals=0),
        compiler_params=pltpu.CompilerParams(vmem_limit_bytes=limit),
        **kwargs,
    )


def lane_sums(block):
    ones = jnp.ones((8, block.shape[1]), jnp.float32)
    return lax.dot_general(
        ones, block, (((1,), (1,)), ((), ())), precision=HIGHEST,
        preferred_element_type=jnp.float32,
    )[0:1]


def column_sum(block):
    rows, width = block.shape
    return jnp.sum(jnp.sum(block.reshape(rows // 8, 8, width), axis=0), axis=0, keepdims=True)


def block_weights(feat, protos, proto_scale, n):
    feat32 = feat.astype(jnp.float32)
    scale = lax.rsqrt(jnp.sum(feat32 * feat32, axis=0, keepdims=True) + EPS)
    scale = jnp.broadcast_to(scale, (8, scale.shape[1])).T[:n, 0:1]
    raw = lax.dot_general(
        feat.T[:n], protos, (((1,), (0,)), ((), ())), preferred_element_type=jnp.float32
    )
    return jnp.exp(raw * scale * proto_scale / TEMP)


def squared_scale(protos):
    wide = protos.astype(jnp.float32)
    return lax.rsqrt(jnp.sum(wide * wide, axis=0, keepdims=True) + EPS)


def weights_body(n, me, feats, protos, weights, col_part, mine):
    npr, ny = feats.shape[0], feats.shape[1]
    values = protos[...]
    proto_scale = squared_scale(values)
    total = jnp.zeros((1, values.shape[1]), jnp.float32)
    for y in range(ny):
        feat = feats[:, y].reshape(npr * feats.shape[2], feats.shape[3])
        block = block_weights(feat, values, proto_scale, n)
        weights[y] = block
        total = total + column_sum(block)
    for z in range(col_part.shape[0]):
        col_part[z] = total
    mine[...] = feats[:, me[0]].reshape(mine.shape)


def row_body(weights, parts, row_part, col_scale):
    total = parts[0]
    for z in range(1, parts.shape[0]):
        total = total + parts[z]
    scale = 1.0 / (K * total)
    col_scale[...] = scale
    ny, n, width = weights.shape
    room = row_part.shape[2] - n
    for y in range(ny):
        acc = weights[y, :, :LANES] * scale[:, :LANES]
        for at in range(LANES, width, LANES):
            acc = acc + weights[y, :, at : at + LANES] * scale[:, at : at + LANES]
        sums = jnp.concatenate([lane_sums(acc), jnp.zeros((1, room), jnp.float32)], axis=1)
        for p in range(row_part.shape[0]):
            row_part[p, y : y + 1, :] = sums


def col_body(total_rows, weights, parts, col_part):
    total = parts[0]
    for y in range(1, parts.shape[0]):
        total = total + parts[y]
    scale = 1.0 / (total_rows * total)
    ny, n, width = weights.shape
    flipped = scale.T
    acc = jnp.zeros((8, width), jnp.float32)
    for y in range(ny):
        block = weights[y] * flipped[:n, y : y + 1]
        acc = acc + jnp.sum(block.reshape(n // 8, 8, width), axis=0)
    total = jnp.sum(acc, axis=0, keepdims=True)
    for z in range(col_part.shape[0]):
        col_part[z] = total


def added(parts):
    total = parts[0]
    for k in range(1, parts.shape[0]):
        total = total + parts[k]
    return total


def relay_body(parts, copies):
    total = added(parts)
    for y in range(copies.shape[0]):
        copies[y] = total


def last_body(parts, col_scale, sent):
    total = added(parts)
    lanes = total.shape[1]
    for y in range(sent.shape[0]):
        sent[y, :, :lanes] = total[y : y + 1]
        sent[y, :, lanes:] = col_scale[...]


def targets_body(total_rows, mine, protos, got, out):
    y = pl.program_id(0)
    n, width = out.shape
    lanes = got.shape[2] - width
    total = got[0, :, :lanes]
    for k in range(1, got.shape[0]):
        total = total + got[k, :, :lanes]
    factor = float(K) * float(total_rows)
    scale = factor * (1.0 / (total_rows * total))
    scale = jnp.broadcast_to(scale, (8, lanes)).T[:n, 0:1]
    values = protos[0]
    block = block_weights(mine[...], values, squared_scale(values), n)
    out[...] = (scale * block * got[y][:, lanes:]).astype(jnp.bfloat16)


def on_device(features, prototypes, masked_index):
    n = masked_index.shape[0]
    ny, nz, npr = lax.axis_size("y"), lax.axis_size("z"), lax.axis_size("p")
    total_rows = n * ny * nz
    k_out = prototypes.shape[0]
    k_own = k_out // ny
    lanes = -(-n // LANES) * LANES
    dim = features.shape[1] * npr
    f32, bf16 = jnp.float32, jnp.bfloat16
    elements = ny * n * k_own

    picks = lax.broadcasted_iota(jnp.int32, (features.shape[0], lanes), 0) == jnp.pad(
        masked_index, (0, lanes - n), constant_values=-1)[None, :]
    chosen = lax.dot_general(
        features, picks.astype(bf16), (((0,), (0,)), ((), ())), preferred_element_type=f32
    ).astype(bf16)
    slices = prototypes.T.reshape(2, ny, k_own // lanes, lanes).transpose(1, 0, 2, 3)
    slices = slices.reshape(ny, -1, lanes)
    held = slices.shape[1]
    both = jnp.concatenate(
        [slices, jnp.broadcast_to(chosen[None], (ny, *chosen.shape))], axis=1)
    both = exchange(both, "y")
    patches = lax.all_gather(both[:, held:], "p")
    protos = from_everyone(both[:, :held].reshape(2 * ny, k_own), "z")
    protos = protos.reshape(nz, ny, 2, k_own).transpose(1, 0, 2, 3).reshape(dim, k_own)
    every_proto = lax.all_gather(protos, "y")

    weights, col_part, mine = call(
        functools.partial(weights_body, n),
        (
            jax.ShapeDtypeStruct((ny, n, k_own), f32),
            jax.ShapeDtypeStruct((nz, 1, k_own), f32),
            jax.ShapeDtypeStruct((dim, lanes), bf16),
        ),
        2 * elements * dim, 4 * elements,
        in_specs=[pl.BlockSpec(memory_space=pltpu.SMEM), VMEM, VMEM],
        out_specs=(VMEM, VMEM, VMEM),
    )(lax.axis_index("y").reshape(1), patches, protos)

    for step in range(ITERS):
        parts = exchange(col_part, "z")
        row_part, col_scale = call(
            row_body,
            (jax.ShapeDtypeStruct((npr, ny, lanes), f32), jax.ShapeDtypeStruct((1, k_own), f32)),
            2 * elements, 4 * elements,
            in_specs=[VMEM, VMEM], out_specs=(VMEM, VMEM),
        )(weights, parts)
        parts = exchange(row_part, "p")
        if step + 1 < ITERS:
            copies = call(
                relay_body, jax.ShapeDtypeStruct((ny, ny, lanes), f32),
                ny * ny * lanes, 8 * ny * ny * lanes, in_specs=[VMEM], out_specs=VMEM,
            )(parts)
            col_part = call(
                functools.partial(col_body, total_rows),
                jax.ShapeDtypeStruct((nz, 1, k_own), f32),
                2 * elements, 4 * elements,
                in_specs=[VMEM, VMEM], out_specs=VMEM,
            )(weights, exchange(copies, "y"))
    sent = call(
        last_body, jax.ShapeDtypeStruct((ny, 1, lanes + k_own), f32),
        ny * ny * lanes, 8 * ny * ny * lanes, in_specs=[VMEM, VMEM], out_specs=VMEM,
    )(parts, col_scale)
    return call(
        functools.partial(targets_body, total_rows),
        jax.ShapeDtypeStruct((n, k_out), bf16),
        2 * elements * dim, 6 * elements,
        grid=(ny,),
        in_specs=[VMEM, pl.BlockSpec((1, dim, k_own), lambda i: (i, 0, 0)), VMEM],
        out_specs=pl.BlockSpec((n, k_own), lambda i: (0, i)),
    )(mine, pltpu.with_memory_space_constraint(every_proto, pltpu.HBM), exchange(sent, "y"))


def solution(mesh):
    rows = mesh.shape["rows"]
    split = Mesh(mesh.devices.reshape(NY, rows // NY, mesh.shape["protos"]), ("y", "z", "p"))
    in_specs = (P(("y", "z"), "p"), P("p", ("y", "z")), P(("y", "z")))
    out_specs = P(("y", "z"), "p")
    return jax.shard_map(
        on_device, mesh=split, in_specs=in_specs, out_specs=out_specs, check_vma=False
    )
```

time: 240 us -> 221 us (0.921)
  other arithmetic: 20.4 us -> 0.01 us
  blocking collectives: 113 us -> 132 us
  Pallas kernels: 0 us -> 15.9 us
  waiting for transfers between devices: 44.7 us -> 32.8 us
  starting transfers between devices: 28.3 us -> 18.6 us
  matrix products: 8.18 us -> 0.19 us
  local copies, waits for them, and re-layouts: 10.5 us -> 6.34 us
    reduce_sum x17 -> x0, other arithmetic: 20.3 us -> none  [the longest x3 9.92 us: on_device(): row_part = jnp.sum(weights * col_scale[None, None, :], axis=2)]
    all_to_all x8 -> x10, blocking collectives: 113 us -> 132 us  [exchange(): return lax.all_to_all(value, axes, split_axis=0, concat_axis=0, tiled=True)]
    pallas_call x0 -> x10, Pallas kernels: none -> 15.9 us  [the longest x1 7.95 us: on_device(): call(functools.partial(targets_body, total_rows), jax.ShapeDtypeStruct((n...]
    all_to_all x3 -> x1, waiting for transfers between devices: 32.6 us -> 20.9 us  [exchange(): return lax.all_to_all(value, axes, split_axis=0, concat_axis=0, tiled=True)]
    all_to_all x3 -> x1, starting transfers between devices: 28.2 us -> 18.5 us  [exchange(): return lax.all_to_all(value, axes, split_axis=0, concat_axis=0, tiled=True)]
    dot_general x3 -> x1, matrix products: 8.18 us -> 0.19 us  [on_device(): lax.dot_general(features, picks.astype(bf16), (((0,), (0,)), ((), ())), p...]
  transfers between devices with their start and end apart: 5 -> 3, of which waited for: 4 -> 2; matrix products, arithmetic and copies ran while one was open for 11% -> 1% of each run, Pallas kernels for 0% -> 4%
where the time goes in v3:
time: 221 us; the launch traced here: 220 us
  blocking collectives  132 us (60%)
  waiting for transfers between devices  32.8 us (15%)
  starting transfers between devices  18.6 us (8%)
  Pallas kernels  15.9 us (7%)
  between operations  13.5 us (6%)
  local copies, waits for them, and re-layouts  6.34 us (3%)
    all_to_all x10, blocking collectives, exchange(): return lax.all_to_all(value, axes, split_axis=0, concat_axis=0, tiled=True)  132 us
    all_to_all x1, waiting for transfers between devices, exchange(): return lax.all_to_all(value, axes, split_axis=0, concat_axis=0, tiled=True)  20.9 us
    all_to_all x1, starting transfers between devices, exchange(): return lax.all_to_all(value, axes, split_axis=0, concat_axis=0, tiled=True)  18.5 us
    all_gather x1, waiting for transfers between devices, on_device(): patches = lax.all_gather(both[:, held:], 'p')  11.9 us
    pallas_call x1, Pallas kernels, on_device(): call(functools.partial(targets_body, total_rows), jax.ShapeDtypeStruct((n...  7.95 us
  transfers between devices with their start and end apart: 3, of which 2 were waited for; matrix products, arithmetic and copies ran while one was open for 1% of the time, Pallas kernels for 4%

profile of v3, /device:TPU:1, one launch (start us, length us, event | category | flops | bytes accessed | tf_op | source)
XLA Modules:
  0.0 219.7 jit_solution(17341368544863024293)
XLA Ops:
  6.5 0.8 reshape.21
  8.3 15.7 %all_to_all.55 = bf16[8,40,256]{2,1,0:T(8,128)(2,1)S(1)} all-to-all(bf16[8,40,256]{2,1,0:T(8,128)(2,1)S(1)} %pad_maximum_fusion), channel_id=1, replica_groups=mesh['y'=8,'z'=16,'p'=8] {'y'}, dimensions={0} | all-to-all | bytes 327680 | tf_op jit(solution)/shard_map/all_to_all | solution.py:23
  24.0 0.9 broadcast_in_dim.5
  24.9 18.5 %all-to-all-start.1 = ((bf16[16,16,1024]{2,1,0:T(8,128)(2,1)}), bf16[16,16,1024]{2,1,0:T(8,128)(2,1)S(1)}, u32[]{:S(2)}, u32[]{:S(2)}) async-start(bf16[16,16,1024]{2,1,0:T(8,128)(2,1)} %broadcast_in_dim.5), calls=%async_computation.1 | async-start | bytes 1048576 | tf_op jit(solution)/shard_map/all_to_all | solution.py:23
  44.2 20.9 %all-to-all-done.1 = bf16[16,16,1024]{2,1,0:T(8,128)(2,1)S(1)} async-done(((bf16[16,16,1024]{2,1,0:T(8,128)(2,1)}), bf16[16,16,1024]{2,1,0:T(8,128)(2,1)S(1)}, u32[]{:S(2)}, u32[]{:S(2)}) %all-to-all-start.1) | async-done | bytes 524320 | tf_op jit(solution)/shard_map/all_to_all | solution.py:23
  66.0 1.0 all_gather_reshape.3
  67.2 11.9 %all-gather.6.cloned.1.call-done = bf16[64,32,256]{2,1,0:T(8,128)(2,1)} async-done(((bf16[8,32,256]{2,1,0:T(8,128)(2,1)}), bf16[64,32,256]{2,1,0:T(8,128)(2,1)}) %all-gather.6.cloned.1.call-update) | async-done | bytes 1048592 | tf_op jit(solution)/shard_map/all_gather | solution.py:175
  79.1 1.2 copy-done.1
  80.3 2.1 shard_map.37
  82.4 24.1 %all_to_all.56.parts = f32[16,1,1024]{2,1,0:T(1,128)S(1)} all-to-all(f32[16,1,1024]{2,1,0:T(1,128)S(1)} %get-tuple-element.14), channel_id=1, replica_groups=mesh['y'=8,'z'=16,'p'=8] {'z'}, dimensions={0} | all-to-all | bytes 131072 | tf_op jit(solution)/shard_map/all_to_all | solution.py:23
  106.6 1.4 shard_map.38
  108.0 9.7 %all_to_all.57.parts = f32[8,8,256]{2,1,0:T(8,128)S(1)} all-to-all(f32[8,8,256]{2,1,0:T(8,128)S(1)} %get-tuple-element.15), channel_id=1, replica_groups=mesh['y'=8,'z'=16,'p'=8] {'p'}, dimensions={0} | all-to-all | bytes 131072 | tf_op jit(solution)/shard_map/all_to_all | solution.py:23
  117.7 14.4 %all_to_all.58.parts = f32[8,8,256]{2,1,0:T(8,128)S(1)} all-to-all(f32[8,8,256]{2,1,0:T(8,128)S(1)} %shard_map.39), channel_id=1, replica_groups=mesh['y'=8,'z'=16,'p'=8] {'y'}, dimensions={0} | all-to-all | bytes 131072 | tf_op jit(solution)/shard_map/all_to_all | solution.py:23
  132.1 0.7 shard_map.40
  132.8 14.3 %all_to_all.59.parts = f32[16,1,1024]{2,1,0:T(1,128)S(1)} all-to-all(f32[16,1,1024]{2,1,0:T(1,128)S(1)} %shard_map.40), channel_id=1, replica_groups=mesh['y'=8,'z'=16,'p'=8] {'z'}, dimensions={0} | all-to-all | bytes 131072 | tf_op jit(solution)/shard_map/all_to_all | solution.py:23
  147.1 1.4 shard_map.41
  148.5 10.5 %all_to_all.60.parts = f32[8,8,256]{2,1,0:T(8,128)S(1)} all-to-all(f32[8,8,256]{2,1,0:T(8,128)S(1)} %get-tuple-element.16), channel_id=1, replica_groups=mesh['y'=8,'z'=16,'p'=8] {'p'}, dimensions={0} | all-to-all | bytes 131072 | tf_op jit(solution)/shard_map/all_to_all | solution.py:23
  159.1 9.7 %all_to_all.61.parts = f32[8,8,256]{2,1,0:T(8,128)S(1)} all-to-all(f32[8,8,256]{2,1,0:T(8,128)S(1)} %shard_map.42), channel_id=1, replica_groups=mesh['y'=8,'z'=16,'p'=8] {'y'}, dimensions={0} | all-to-all | bytes 131072 | tf_op jit(solution)/shard_map/all_to_all | solution.py:23
  168.8 0.7 shard_map.43
  169.5 14.2 %all_to_all.62.parts = f32[16,1,1024]{2,1,0:T(1,128)S(1)} all-to-all(f32[16,1,1024]{2,1,0:T(1,128)S(1)} %shard_map.43), channel_id=1, replica_groups=mesh['y'=8,'z'=16,'p'=8] {'z'}, dimensions={0} | all-to-all | bytes 131072 | tf_op jit(solution)/shard_map/all_to_all | solution.py:23
  183.8 1.4 shard_map.44
  185.2 10.4 %all_to_all.63.parts = f32[8,8,256]{2,1,0:T(8,128)S(1)} all-to-all(f32[8,8,256]{2,1,0:T(8,128)S(1)} %get-tuple-element.17), channel_id=1, replica_groups=mesh['y'=8,'z'=16,'p'=8] {'p'}, dimensions={0} | all-to-all | bytes 131072 | tf_op jit(solution)/shard_map/all_to_all | solution.py:23
  195.6 9.3 %all_to_all.64.got = f32[8,1,1280]{2,1,0:T(1,128)S(1)} all-to-all(f32[8,1,1280]{2,1,0:T(1,128)S(1)} %shard_map.45), channel_id=1, replica_groups=mesh['y'=8,'z'=16,'p'=8] {'y'}, dimensions={0} | all-to-all | bytes 81920 | tf_op jit(solution)/shard_map/all_to_all | solution.py:23
  205.0 8.0 %shard_map.46 = bf16[192,8192]{1,0:T(8,128)(2,1)} custom-call(bf16[256,256]{1,0:T(8,128)(2,1)S(1)} %get-tuple-element.12.mine, bf16[8,256,1024]{2,1,0:T(8,128)(2,1)} %all-gather.4.cloned.1.call-done.protos, f32[8,1,1280]{2,1,0:T(1,128)S(1)} %all_to_all.64.got), custom_call_target="tpu_custom_call" | custom-call | flops 805306368 | bytes 9437184 | tf_op jit(solution)/shard_map/pallas_call | solution.py:216
  (23 shorter events, 2.8 us)
Async XLA Ops:
  6.5 1.5 copy-start
  24.9 40.2 %all-to-all-start.1 = ((bf16[16,16,1024]{2,1,0:T(8,128)(2,1)}), bf16[16,16,1024]{2,1,0:T(8,128)(2,1)S(1)}, u32[]{:S(2)}, u32[]{:S(2)}) async-start(bf16[16,16,1024]{2,1,0:T(8,128)(2,1)} %broadcast_in_dim.5), calls=%async_computation.1 | async-start | bytes 1048576 | tf_op jit(solution)/shard_map/all_to_all | solution.py:23
  43.4 35.6 %all-gather.6.cloned.1.call-start = ((), (), s32[]{:S(2)}) async-start(), calls=%async_computation.12 | async-start | bytes 1179648 | tf_op jit(solution)/shard_map/all_gather | solution.py:175
  44.2 160.8 %all-gather.4.cloned.1.call-start = ((), (), s32[]{:S(2)}) async-start(), calls=%async_computation.11 | async-start | bytes 4718592 | tf_op jit(solution)/shard_map/all_gather | solution.py:178
  79.1 1.2 copy-start.1
Sparse Core Ops, SparseCore 0:
  47.0 32.0 all-gather.5
  81.7 63.3 all-gather.3

commit v4 on v3

--- a/solution.py
+++ b/solution.py
@@ -46,39 +46,45 @@
     )[0:1]
 
 
-def column_sum(block):
-    rows, width = block.shape
-    return jnp.sum(jnp.sum(block.reshape(rows // 8, 8, width), axis=0), axis=0, keepdims=True)
-
-
-def block_weights(feat, protos, proto_scale, n):
-    feat32 = feat.astype(jnp.float32)
-    scale = lax.rsqrt(jnp.sum(feat32 * feat32, axis=0, keepdims=True) + EPS)
-    scale = jnp.broadcast_to(scale, (8, scale.shape[1])).T[:n, 0:1]
-    raw = lax.dot_general(
-        feat.T[:n], protos, (((1,), (0,)), ((), ())), preferred_element_type=jnp.float32
-    )
-    return jnp.exp(raw * scale * proto_scale / TEMP)
-
-
 def squared_scale(protos):
     wide = protos.astype(jnp.float32)
     return lax.rsqrt(jnp.sum(wide * wide, axis=0, keepdims=True) + EPS)
 
 
-def weights_body(n, me, feats, protos, weights, col_part, mine):
-    npr, ny = feats.shape[0], feats.shape[1]
+def block_weights(feat, feat_scale, protos):
+    proto_scale = squared_scale(protos)
+    raw = lax.dot_general(
+        feat, protos, (((1,), (0,)), ((), ())), preferred_element_type=jnp.float32
+    )
+    parts = []
+    for at in range(0, raw.shape[1], LANES):
+        part = raw[:, at : at + LANES] * feat_scale * proto_scale[:, at : at + LANES]
+        parts.append(jnp.exp(part / TEMP))
+    return jnp.concatenate(parts, axis=1)
+
+
+def feats_body(me, patches, feats, scales, mine, mine_scale):
+    npr, ny, share, lanes = patches.shape
+    n = feats.shape[1]
+    for y in range(ny):
+        feat = patches[:, y].reshape(npr * share, lanes)
+        scale = jnp.broadcast_to(squared_scale(feat), (LANES, lanes)).T
+        feats[y] = feat.T[:n]
+        scales[y] = scale[:n]
+    mine[...] = feats[me[0]]
+    mine_scale[...] = scales[me[0]]
+
+
+def weights_body(feats, scales, protos, weights, col_part):
     values = protos[...]
-    proto_scale = squared_scale(values)
-    total = jnp.zeros((1, values.shape[1]), jnp.float32)
-    for y in range(ny):
-        feat = feats[:, y].reshape(npr * feats.shape[2], feats.shape[3])
-        block = block_weights(feat, values, proto_scale, n)
+    total = jnp.zeros((8, values.shape[1]), jnp.float32)
+    for y in range(feats.shape[0]):
+        block = block_weights(feats[y], scales[y], values)
         weights[y] = block
-        total = total + column_sum(block)
+        total = total + jnp.sum(block.reshape(-1, 8, block.shape[1]), axis=0)
+    total = jnp.sum(total, axis=0, keepdims=True)
     for z in range(col_part.shape[0]):
         col_part[z] = total
-    mine[...] = feats[:, me[0]].reshape(mine.shape)
 
 
 def row_body(weights, parts, row_part, col_scale):
@@ -127,7 +133,7 @@
         copies[y] = total
 
 
-def last_body(parts, col_scale, sent):
+def last_body(parts, col_scale, every_proto, sent):
     total = added(parts)
     lanes = total.shape[1]
     for y in range(sent.shape[0]):
@@ -135,7 +141,7 @@
         sent[y, :, lanes:] = col_scale[...]
 
 
-def targets_body(total_rows, mine, protos, got, out):
+def targets_body(total_rows, mine, mine_scale, protos, got, out):
     y = pl.program_id(0)
     n, width = out.shape
     lanes = got.shape[2] - width
@@ -145,8 +151,7 @@
     factor = float(K) * float(total_rows)
     scale = factor * (1.0 / (total_rows * total))
     scale = jnp.broadcast_to(scale, (8, lanes)).T[:n, 0:1]
-    values = protos[0]
-    block = block_weights(mine[...], values, squared_scale(values), n)
+    block = block_weights(mine[...], mine_scale[...], protos[y])
     out[...] = (scale * block * got[y][:, lanes:]).astype(jnp.bfloat16)
 
 
@@ -174,20 +179,30 @@
     both = exchange(both, "y")
     patches = lax.all_gather(both[:, held:], "p")
     protos = from_everyone(both[:, :held].reshape(2 * ny, k_own), "z")
+    prepared = call(
+        feats_body,
+        (
+            jax.ShapeDtypeStruct((ny, n, dim), bf16),
+            jax.ShapeDtypeStruct((ny, n, LANES), f32),
+            jax.ShapeDtypeStruct((n, dim), bf16),
+            jax.ShapeDtypeStruct((n, LANES), f32),
+        ),
+        2 * ny * lanes * dim, 4 * ny * lanes * dim,
+        in_specs=[pl.BlockSpec(memory_space=pltpu.SMEM), VMEM],
+        out_specs=(VMEM, VMEM, VMEM, VMEM),
+    )(lax.axis_index("y").reshape(1), patches)
     protos = protos.reshape(nz, ny, 2, k_own).transpose(1, 0, 2, 3).reshape(dim, k_own)
+    feats, scales, mine, mine_scale = prepared
     every_proto = lax.all_gather(protos, "y")
-
-    weights, col_part, mine = call(
-        functools.partial(weights_body, n),
+    weights, col_part = call(
+        weights_body,
         (
             jax.ShapeDtypeStruct((ny, n, k_own), f32),
             jax.ShapeDtypeStruct((nz, 1, k_own), f32),
-            jax.ShapeDtypeStruct((dim, lanes), bf16),
         ),
         2 * elements * dim, 4 * elements,
-        in_specs=[pl.BlockSpec(memory_space=pltpu.SMEM), VMEM, VMEM],
-        out_specs=(VMEM, VMEM, VMEM),
-    )(lax.axis_index("y").reshape(1), patches, protos)
+        in_specs=[VMEM, VMEM, VMEM], out_specs=(VMEM, VMEM),
+    )(feats, scales, protos)
 
     for step in range(ITERS):
         parts = exchange(col_part, "z")
@@ -211,16 +226,16 @@
             )(weights, exchange(copies, "y"))
     sent = call(
         last_body, jax.ShapeDtypeStruct((ny, 1, lanes + k_own), f32),
-        ny * ny * lanes, 8 * ny * ny * lanes, in_specs=[VMEM, VMEM], out_specs=VMEM,
-    )(parts, col_scale)
+        ny * ny * lanes, 8 * ny * ny * lanes, in_specs=[VMEM, VMEM, pl.BlockSpec(memory_space=pl.ANY)], out_specs=VMEM,
+    )(parts, col_scale, pltpu.with_memory_space_constraint(every_proto, pltpu.HBM))
     return call(
         functools.partial(targets_body, total_rows),
         jax.ShapeDtypeStruct((n, k_out), bf16),
         2 * elements * dim, 6 * elements,
         grid=(ny,),
-        in_specs=[VMEM, pl.BlockSpec((1, dim, k_own), lambda i: (i, 0, 0)), VMEM],
+        in_specs=[VMEM, VMEM, VMEM, VMEM],
         out_specs=pl.BlockSpec((n, k_own), lambda i: (0, i)),
-    )(mine, pltpu.with_memory_space_constraint(every_proto, pltpu.HBM), exchange(sent, "y"))
+    )(mine, mine_scale, every_proto, exchange(sent, "y"))
 
 
 def solution(mesh):

time: 221 us -> 218 us (0.986)
  Pallas kernels: 15.9 us -> 13 us
    pallas_call x1, Pallas kernels: 7.95 us -> 4.92 us  [on_device(): call(functools.partial(targets_body, total_rows), jax.ShapeDtypeStruct((n...]
where the time goes in v4:
time: 218 us; the launch traced here: 217 us
  blocking collectives  133 us (61%)
  waiting for transfers between devices  33 us (15%)
  starting transfers between devices  18.6 us (9%)
  between operations  13.5 us (6%)
  Pallas kernels  13 us (6%)
  local copies, waits for them, and re-layouts  6.35 us (3%)
    all_to_all x10, blocking collectives, exchange(): return lax.all_to_all(value, axes, split_axis=0, concat_axis=0, tiled=True)  133 us
    all_to_all x1, waiting for transfers between devices, exchange(): return lax.all_to_all(value, axes, split_axis=0, concat_axis=0, tiled=True)  20.9 us
    all_to_all x1, starting transfers between devices, exchange(): return lax.all_to_all(value, axes, split_axis=0, concat_axis=0, tiled=True)  18.5 us
    all_gather x1, waiting for transfers between devices, on_device(): patches = lax.all_gather(both[:, held:], 'p')  12.1 us
    pallas_call x1, Pallas kernels, on_device(): call(functools.partial(targets_body, total_rows), jax.ShapeDtypeStruct((n...  4.92 us
  transfers between devices with their start and end apart: 3, of which 2 were waited for; matrix products, arithmetic and copies ran while one was open for 1% of the time, Pallas kernels for 4%

profile of v4, /device:TPU:1, one launch (start us, length us, event | category | flops | bytes accessed | tf_op | source)
XLA Modules:
  0.0 217.3 jit_solution(12087618980686710698)
XLA Ops:
  6.5 0.8 reshape.21
  7.4 0.7 pad.4
  8.3 15.7 %all_to_all.55 = bf16[8,40,256]{2,1,0:T(8,128)(2,1)S(1)} all-to-all(bf16[8,40,256]{2,1,0:T(8,128)(2,1)S(1)} %pad_maximum_fusion), channel_id=1, replica_groups=mesh['y'=8,'z'=16,'p'=8] {'y'}, dimensions={0} | all-to-all | bytes 327680 | tf_op jit(solution)/shard_map/all_to_all | solution.py:23
  24.0 0.9 broadcast_in_dim.5
  24.9 18.5 %all-to-all-start.1 = ((bf16[16,16,1024]{2,1,0:T(8,128)(2,1)}), bf16[16,16,1024]{2,1,0:T(8,128)(2,1)S(1)}, u32[]{:S(2)}, u32[]{:S(2)}) async-start(bf16[16,16,1024]{2,1,0:T(8,128)(2,1)} %broadcast_in_dim.5), calls=%async_computation.1 | async-start | bytes 1048576 | tf_op jit(solution)/shard_map/all_to_all | solution.py:23
  44.2 20.9 %all-to-all-done.1 = bf16[16,16,1024]{2,1,0:T(8,128)(2,1)S(1)} async-done(((bf16[16,16,1024]{2,1,0:T(8,128)(2,1)}), bf16[16,16,1024]{2,1,0:T(8,128)(2,1)S(1)}, u32[]{:S(2)}, u32[]{:S(2)}) %all-to-all-start.1) | async-done | bytes 524320 | tf_op jit(solution)/shard_map/all_to_all | solution.py:23
  66.0 1.0 all_gather_reshape.3
  67.0 12.1 %all-gather.6.cloned.1.call-done = bf16[64,32,256]{2,1,0:T(8,128)(2,1)} async-done(((bf16[8,32,256]{2,1,0:T(8,128)(2,1)}), bf16[64,32,256]{2,1,0:T(8,128)(2,1)}) %all-gather.6.cloned.1.call-update) | async-done | bytes 1048592 | tf_op jit(solution)/shard_map/all_gather | solution.py:180
  79.1 1.2 copy-done.2
  80.3 0.7 shard_map.37
  81.2 1.6 shard_map.38
  82.9 24.1 %all_to_all.56.parts = f32[16,1,1024]{2,1,0:T(1,128)S(1)} all-to-all(f32[16,1,1024]{2,1,0:T(1,128)S(1)} %get-tuple-element.20), channel_id=1, replica_groups=mesh['y'=8,'z'=16,'p'=8] {'z'}, dimensions={0} | all-to-all | bytes 131072 | tf_op jit(solution)/shard_map/all_to_all | solution.py:23
  107.0 1.4 shard_map.39
  108.5 9.7 %all_to_all.57.parts = f32[8,8,256]{2,1,0:T(8,128)S(1)} all-to-all(f32[8,8,256]{2,1,0:T(8,128)S(1)} %get-tuple-element.21), channel_id=1, replica_groups=mesh['y'=8,'z'=16,'p'=8] {'p'}, dimensions={0} | all-to-all | bytes 131072 | tf_op jit(solution)/shard_map/all_to_all | solution.py:23
  118.2 14.4 %all_to_all.58.parts = f32[8,8,256]{2,1,0:T(8,128)S(1)} all-to-all(f32[8,8,256]{2,1,0:T(8,128)S(1)} %shard_map.40), channel_id=1, replica_groups=mesh['y'=8,'z'=16,'p'=8] {'y'}, dimensions={0} | all-to-all | bytes 131072 | tf_op jit(solution)/shard_map/all_to_all | solution.py:23
  133.2 14.2 %all_to_all.59.parts = f32[16,1,1024]{2,1,0:T(1,128)S(1)} all-to-all(f32[16,1,1024]{2,1,0:T(1,128)S(1)} %shard_map.41), channel_id=1, replica_groups=mesh['y'=8,'z'=16,'p'=8] {'z'}, dimensions={0} | all-to-all | bytes 131072 | tf_op jit(solution)/shard_map/all_to_all | solution.py:23
  147.5 1.4 shard_map.42
  148.9 10.5 %all_to_all.60.parts = f32[8,8,256]{2,1,0:T(8,128)S(1)} all-to-all(f32[8,8,256]{2,1,0:T(8,128)S(1)} %get-tuple-element.22), channel_id=1, replica_groups=mesh['y'=8,'z'=16,'p'=8] {'p'}, dimensions={0} | all-to-all | bytes 131072 | tf_op jit(solution)/shard_map/all_to_all | solution.py:23
  159.4 9.7 %all_to_all.61.parts = f32[8,8,256]{2,1,0:T(8,128)S(1)} all-to-all(f32[8,8,256]{2,1,0:T(8,128)S(1)} %shard_map.43), channel_id=1, replica_groups=mesh['y'=8,'z'=16,'p'=8] {'y'}, dimensions={0} | all-to-all | bytes 131072 | tf_op jit(solution)/shard_map/all_to_all | solution.py:23
  169.8 14.2 %all_to_all.62.parts = f32[16,1,1024]{2,1,0:T(1,128)S(1)} all-to-all(f32[16,1,1024]{2,1,0:T(1,128)S(1)} %shard_map.44), channel_id=1, replica_groups=mesh['y'=8,'z'=16,'p'=8] {'z'}, dimensions={0} | all-to-all | bytes 131072 | tf_op jit(solution)/shard_map/all_to_all | solution.py:23
  184.1 1.4 shard_map.45
  185.5 10.4 %all_to_all.63.parts = f32[8,8,256]{2,1,0:T(8,128)S(1)} all-to-all(f32[8,8,256]{2,1,0:T(8,128)S(1)} %get-tuple-element.23), channel_id=1, replica_groups=mesh['y'=8,'z'=16,'p'=8] {'p'}, dimensions={0} | all-to-all | bytes 131072 | tf_op jit(solution)/shard_map/all_to_all | solution.py:23
  195.9 9.6 %all_to_all.64.got = f32[8,1,1280]{2,1,0:T(1,128)S(1)} all-to-all(f32[8,1,1280]{2,1,0:T(1,128)S(1)} %shard_map.46), channel_id=1, replica_groups=mesh['y'=8,'z'=16,'p'=8] {'y'}, dimensions={0} | all-to-all | bytes 81920 | tf_op jit(solution)/shard_map/all_to_all | solution.py:23
  205.5 4.9 %shard_map.47 = bf16[192,8192]{1,0:T(8,128)(2,1)} custom-call(bf16[192,256]{1,0:T(8,128)(2,1)S(1)} %get-tuple-element.15.mine, f32[192,128]{1,0:T(8,128)S(1)} %get-tuple-element.16.mine_scale, bf16[8,256,1024]{2,1,0:T(8,128)(2,1)S(1)} %copy-done.1, f32[8,1,1280]{2,1,0:T(1,128)S(1)} %all_to_all.64.got), custom_call_target="tpu_custom_call" | custom-call | flops 805306368 | bytes 9437184 | tf_op jit(solution)/shard_map/pallas_call | solution.py:231
  (26 shorter events, 3.5 us)
Async XLA Ops:
  6.5 1.5 copy-start
  24.9 40.2 %all-to-all-start.1 = ((bf16[16,16,1024]{2,1,0:T(8,128)(2,1)}), bf16[16,16,1024]{2,1,0:T(8,128)(2,1)S(1)}, u32[]{:S(2)}, u32[]{:S(2)}) async-start(bf16[16,16,1024]{2,1,0:T(8,128)(2,1)} %broadcast_in_dim.5), calls=%async_computation.1 | async-start | bytes 1048576 | tf_op jit(solution)/shard_map/all_to_all | solution.py:23
  43.4 35.6 %all-gather.6.cloned.1.call-start = ((), (), s32[]{:S(2)}) async-start(), calls=%async_computation.12 | async-start | bytes 1179648 | tf_op jit(solution)/shard_map/all_gather | solution.py:180
  44.2 151.7 %all-gather.4.cloned.1.call-start = ((), (), s32[]{:S(2)}) async-start(), calls=%async_computation.11 | async-start | bytes 4718592 | tf_op jit(solution)/shard_map/all_gather | solution.py:196
  79.1 1.2 copy-start.2
  195.9 9.6 %copy-start.1 = (bf16[8,256,1024]{2,1,0:T(8,128)(2,1)S(1)}, bf16[8,256,1024]{2,1,0:T(8,128)(2,1)}, u32[]{:S(2)}) copy-start(bf16[8,256,1024]{2,1,0:T(8,128)(2,1)} %all-gather.4.cloned.1.call-done.every_proto.protos) | copy-start | bytes 12582916
Sparse Core Ops, SparseCore 0:
  47.0 32.0 all-gather.5
  81.7 63.3 all-gather.3

commit v5 on v4

--- a/solution.py
+++ b/solution.py
@@ -16,7 +16,6 @@
 NY = 8
 LANES = 128
 VMEM = pl.BlockSpec(memory_space=pltpu.VMEM)
-HIGHEST = lax.Precision.HIGHEST
 
 
 def exchange(value, axes):
@@ -26,6 +25,10 @@
 def from_everyone(value, axes):
     copies = jnp.broadcast_to(value, (lax.axis_size(axes), *value.shape))
     return exchange(copies, axes)
+
+
+def in_hbm(value):
+    return pltpu.with_memory_space_constraint(value, pltpu.HBM)
 
 
 def call(body, out_shape, flops, moved, limit=20 * 2**20, **kwargs):
@@ -38,12 +41,27 @@
     )
 
 
-def lane_sums(block):
-    ones = jnp.ones((8, block.shape[1]), jnp.float32)
-    return lax.dot_general(
-        ones, block, (((1,), (1,)), ((), ())), precision=HIGHEST,
-        preferred_element_type=jnp.float32,
-    )[0:1]
+def lane_sums(block, lanes):
+    empty = jnp.zeros((lanes - block.shape[0], block.shape[1]), jnp.float32)
+    return jnp.sum(jnp.concatenate([block, empty], axis=0).T, axis=0, keepdims=True)
+
+
+def first_body(features, protos, index, both):
+    ny, rows, lanes = both.shape
+    share, count = features.shape
+    n = index.shape[1]
+    index = jnp.concatenate([index[...], jnp.full((1, lanes - n), -1, jnp.int32)], axis=1)
+    picks = lax.broadcasted_iota(jnp.int32, (count, lanes), 0) == index
+    chosen = lax.dot_general(
+        features[...], picks.astype(jnp.float32).astype(jnp.bfloat16),
+        (((1,), (0,)), ((), ())), preferred_element_type=jnp.float32,
+    ).astype(jnp.bfloat16)
+    held = rows - share
+    for y in range(ny):
+        for at in range(0, held, 2):
+            start = (y * held // 2 + at // 2) * lanes
+            both[y, at : at + 2, :] = protos[:, start : start + lanes]
+        both[y, held:, :] = chosen
 
 
 def squared_scale(protos):
@@ -63,14 +81,26 @@
     return jnp.concatenate(parts, axis=1)
 
 
-def feats_body(me, patches, feats, scales, mine, mine_scale):
+def arrival_order(ny, nz):
+    dim = 2 * ny * nz
+    at = lax.broadcasted_iota(jnp.int32, (dim, dim), 0)
+    low, mid = at & 1, (at >> 1) & (nz - 1)
+    high = at >> nz.bit_length()
+    target = mid * (2 * ny) + high * 2 + low
+    hit = lax.broadcasted_iota(jnp.int32, (dim, dim), 1) == target
+    return hit.astype(jnp.float32).astype(jnp.bfloat16)
+
+
+def feats_body(nz, me, patches, feats, scales, mine, mine_scale):
     npr, ny, share, lanes = patches.shape
     n = feats.shape[1]
+    order = arrival_order(ny, nz)
     for y in range(ny):
         feat = patches[:, y].reshape(npr * share, lanes)
-        scale = jnp.broadcast_to(squared_scale(feat), (LANES, lanes)).T
-        feats[y] = feat.T[:n]
-        scales[y] = scale[:n]
+        scales[y] = jnp.broadcast_to(squared_scale(feat), (LANES, lanes)).T[:n]
+        feats[y] = lax.dot_general(
+            feat.T[:n], order, (((1,), (0,)), ((), ())), preferred_element_type=jnp.float32
+        ).astype(jnp.bfloat16)
     mine[...] = feats[me[0]]
     mine_scale[...] = scales[me[0]]
 
@@ -93,13 +123,12 @@
         total = total + parts[z]
     scale = 1.0 / (K * total)
     col_scale[...] = scale
-    ny, n, width = weights.shape
-    room = row_part.shape[2] - n
+    ny, _, width = weights.shape
     for y in range(ny):
         acc = weights[y, :, :LANES] * scale[:, :LANES]
         for at in range(LANES, width, LANES):
             acc = acc + weights[y, :, at : at + LANES] * scale[:, at : at + LANES]
-        sums = jnp.concatenate([lane_sums(acc), jnp.zeros((1, room), jnp.float32)], axis=1)
+        sums = lane_sums(acc, row_part.shape[2])
         for p in range(row_part.shape[0]):
             row_part[p, y : y + 1, :] = sums
 
@@ -141,18 +170,29 @@
         sent[y, :, lanes:] = col_scale[...]
 
 
-def targets_body(total_rows, mine, mine_scale, protos, got, out):
-    y = pl.program_id(0)
-    n, width = out.shape
+def targets_body(total_rows, mine, mine_scale, protos, got, out, row_scale):
+    step = pl.program_id(0)
+    n = out.shape[0]
+    width = protos.shape[2]
     lanes = got.shape[2] - width
-    total = got[0, :, :lanes]
-    for k in range(1, got.shape[0]):
-        total = total + got[k, :, :lanes]
-    factor = float(K) * float(total_rows)
-    scale = factor * (1.0 / (total_rows * total))
-    scale = jnp.broadcast_to(scale, (8, lanes)).T[:n, 0:1]
-    block = block_weights(mine[...], mine_scale[...], protos[y])
-    out[...] = (scale * block * got[y][:, lanes:]).astype(jnp.bfloat16)
+
+    @pl.when(step == 0)
+    def _():
+        total = got[0, :, :lanes]
+        for k in range(1, got.shape[0]):
+            total = total + got[k, :, :lanes]
+        factor = float(K) * float(total_rows)
+        scale = factor * (1.0 / (total_rows * total))
+        row_scale[...] = jnp.broadcast_to(scale, (LANES, lanes)).T[:n]
+
+    count = out.shape[1] // width
+    for k in range(count):
+        y = step * count + k
+        block = block_weights(mine[...], mine_scale[...], protos[y])
+        col_scale = got[y][:, lanes:]
+        for at in range(0, width, LANES):
+            part = row_scale[...] * block[:, at : at + LANES] * col_scale[:, at : at + LANES]
+            out[:, k * width + at : k * width + at + LANES] = part.astype(jnp.bfloat16)
 
 
 def on_device(features, prototypes, masked_index):
@@ -166,21 +206,26 @@
     f32, bf16 = jnp.float32, jnp.bfloat16
     elements = ny * n * k_own
 
-    picks = lax.broadcasted_iota(jnp.int32, (features.shape[0], lanes), 0) == jnp.pad(
-        masked_index, (0, lanes - n), constant_values=-1)[None, :]
-    chosen = lax.dot_general(
-        features, picks.astype(bf16), (((0,), (0,)), ((), ())), preferred_element_type=f32
-    ).astype(bf16)
-    slices = prototypes.T.reshape(2, ny, k_own // lanes, lanes).transpose(1, 0, 2, 3)
-    slices = slices.reshape(ny, -1, lanes)
-    held = slices.shape[1]
-    both = jnp.concatenate(
-        [slices, jnp.broadcast_to(chosen[None], (ny, *chosen.shape))], axis=1)
+    share = features.shape[1]
+    held = 2 * k_own // lanes
+    both = call(
+        first_body, jax.ShapeDtypeStruct((ny, held + share, lanes), bf16),
+        2 * share * lanes * features.shape[0], 4 * ny * share * lanes,
+        grid=(1,),
+        in_specs=[
+            pl.BlockSpec((share, features.shape[0]), lambda i: (0, 0)),
+            pl.BlockSpec((2, k_out), lambda i: (0, 0)),
+            pl.BlockSpec((1, n), lambda i: (0, 0)),
+        ],
+        out_specs=VMEM,
+    )(in_hbm(features.T), in_hbm(prototypes.T), in_hbm(masked_index.reshape(1, n)))
     both = exchange(both, "y")
+    pieces = both[:, :held].reshape(ny, held // 2, 2, lanes).transpose(0, 2, 1, 3)
+    pieces = pieces.reshape(2 * ny, k_own)
     patches = lax.all_gather(both[:, held:], "p")
-    protos = from_everyone(both[:, :held].reshape(2 * ny, k_own), "z")
+    protos = from_everyone(pieces, "z").reshape(dim, k_own)
     prepared = call(
-        feats_body,
+        functools.partial(feats_body, nz),
         (
             jax.ShapeDtypeStruct((ny, n, dim), bf16),
             jax.ShapeDtypeStruct((ny, n, LANES), f32),
@@ -191,7 +236,6 @@
         in_specs=[pl.BlockSpec(memory_space=pltpu.SMEM), VMEM],
         out_specs=(VMEM, VMEM, VMEM, VMEM),
     )(lax.axis_index("y").reshape(1), patches)
-    protos = protos.reshape(nz, ny, 2, k_own).transpose(1, 0, 2, 3).reshape(dim, k_own)
     feats, scales, mine, mine_scale = prepared
     every_proto = lax.all_gather(protos, "y")
     weights, col_part = call(
@@ -227,14 +271,15 @@
     sent = call(
         last_body, jax.ShapeDtypeStruct((ny, 1, lanes + k_own), f32),
         ny * ny * lanes, 8 * ny * ny * lanes, in_specs=[VMEM, VMEM, pl.BlockSpec(memory_space=pl.ANY)], out_specs=VMEM,
-    )(parts, col_scale, pltpu.with_memory_space_constraint(every_proto, pltpu.HBM))
+    )(parts, col_scale, in_hbm(every_proto))
     return call(
         functools.partial(targets_body, total_rows),
         jax.ShapeDtypeStruct((n, k_out), bf16),
         2 * elements * dim, 6 * elements,
-        grid=(ny,),
+        grid=(ny // 2,),
         in_specs=[VMEM, VMEM, VMEM, VMEM],
-        out_specs=pl.BlockSpec((n, k_own), lambda i: (0, i)),
+        out_specs=pl.BlockSpec((n, 2 * k_own), lambda i: (0, i)),
+        scratch_shapes=[pltpu.VMEM((n, LANES), f32)],
     )(mine, mine_scale, every_proto, exchange(sent, "y"))
 
 

time: 218 us -> 215 us (0.986)
  Pallas kernels: 13 us -> 10.5 us
    pallas_call x3, Pallas kernels: 4.28 us -> 1.92 us  [on_device(): call(row_body, (jax.ShapeDtypeStruct((npr, ny, lanes), f32), jax.ShapeDty...]
  transfers between devices with their start and end apart: 3 -> 3, of which waited for: 2 -> 2; matrix products, arithmetic and copies ran while one was open for 1% -> 0% of each run, Pallas kernels for 4% -> 3%
where the time goes in v5:
time: 215 us; the launch traced here: 214 us
  blocking collectives  133 us (62%)
  waiting for transfers between devices  34 us (16%)
  starting transfers between devices  18.6 us (9%)
  between operations  13.5 us (6%)
  Pallas kernels  10.5 us (5%)
  local copies, waits for them, and re-layouts  4.65 us (2%)
    all_to_all x10, blocking collectives, exchange(): return lax.all_to_all(value, axes, split_axis=0, concat_axis=0, tiled=True)  133 us
    all_to_all x1, waiting for transfers between devices, exchange(): return lax.all_to_all(value, axes, split_axis=0, concat_axis=0, tiled=True)  20.9 us
    all_to_all x1, starting transfers between devices, exchange(): return lax.all_to_all(value, axes, split_axis=0, concat_axis=0, tiled=True)  18.5 us
    all_gather x1, waiting for transfers between devices, on_device(): patches = lax.all_gather(both[:, held:], 'p')  13.1 us
  transfers between devices with their start and end apart: 3, of which 2 were waited for; matrix products, arithmetic and copies ran while one was open for 0% of the time, Pallas kernels for 3%

profile of v5, /device:TPU:1, one launch (start us, length us, event | category | flops | bytes accessed | tf_op | source)
XLA Modules:
  0.0 213.9 jit_solution(13979857328876307209)
XLA Ops:
  6.5 0.9 shard_map.37
  7.5 15.7 %all_to_all.55 = bf16[8,40,256]{2,1,0:T(8,128)(2,1)S(1)} all-to-all(bf16[8,40,256]{2,1,0:T(8,128)(2,1)S(1)} %shard_map.37), channel_id=1, replica_groups=mesh['y'=8,'z'=16,'p'=8] {'y'}, dimensions={0} | all-to-all | bytes 327680 | tf_op jit(solution)/shard_map/all_to_all | solution.py:22
  23.3 0.9 broadcast_in_dim.3
  24.1 18.5 %all-to-all-start.1 = ((bf16[16,16,1024]{2,1,0:T(8,128)(2,1)}), bf16[16,16,1024]{2,1,0:T(8,128)(2,1)S(1)}, u32[]{:S(2)}, u32[]{:S(2)}) async-start(bf16[16,16,1024]{2,1,0:T(8,128)(2,1)} %broadcast_in_dim.3), calls=%async_computation.1 | async-start | bytes 1048576 | tf_op jit(solution)/shard_map/all_to_all | solution.py:22
  42.7 0.7 slice.8
  43.5 20.9 %all-to-all-done.1 = bf16[16,16,1024]{2,1,0:T(8,128)(2,1)S(1)} async-done(((bf16[16,16,1024]{2,1,0:T(8,128)(2,1)}), bf16[16,16,1024]{2,1,0:T(8,128)(2,1)S(1)}, u32[]{:S(2)}, u32[]{:S(2)}) %all-to-all-start.1) | async-done | bytes 524320 | tf_op jit(solution)/shard_map/all_to_all | solution.py:22
  64.3 0.8 copy-done.1
  65.1 13.1 %all-gather.6.cloned.1.call-done = bf16[64,32,256]{2,1,0:T(8,128)(2,1)} async-done(((bf16[8,32,256]{2,1,0:T(8,128)(2,1)}), bf16[64,32,256]{2,1,0:T(8,128)(2,1)}) %all-gather.6.cloned.1.call-update) | async-done | bytes 1048592 | tf_op jit(solution)/shard_map/all_gather | solution.py:225
  78.3 1.2 copy-done.3
  79.5 0.8 shard_map.38
  80.3 1.0 copy-done.2
  81.3 1.6 shard_map.39
  83.0 24.1 %all_to_all.56.parts = f32[16,1,1024]{2,1,0:T(1,128)S(1)} all-to-all(f32[16,1,1024]{2,1,0:T(1,128)S(1)} %get-tuple-element.20), channel_id=1, replica_groups=mesh['y'=8,'z'=16,'p'=8] {'z'}, dimensions={0} | all-to-all | bytes 131072 | tf_op jit(solution)/shard_map/all_to_all | solution.py:22
  107.1 0.7 shard_map.40
  107.8 9.7 %all_to_all.57.parts = f32[8,8,256]{2,1,0:T(8,128)S(1)} all-to-all(f32[8,8,256]{2,1,0:T(8,128)S(1)} %get-tuple-element.21), channel_id=1, replica_groups=mesh['y'=8,'z'=16,'p'=8] {'p'}, dimensions={0} | all-to-all | bytes 131072 | tf_op jit(solution)/shard_map/all_to_all | solution.py:22
  117.5 14.4 %all_to_all.58.parts = f32[8,8,256]{2,1,0:T(8,128)S(1)} all-to-all(f32[8,8,256]{2,1,0:T(8,128)S(1)} %shard_map.41), channel_id=1, replica_groups=mesh['y'=8,'z'=16,'p'=8] {'y'}, dimensions={0} | all-to-all | bytes 131072 | tf_op jit(solution)/shard_map/all_to_all | solution.py:22
  132.5 14.2 %all_to_all.59.parts = f32[16,1,1024]{2,1,0:T(1,128)S(1)} all-to-all(f32[16,1,1024]{2,1,0:T(1,128)S(1)} %shard_map.42), channel_id=1, replica_groups=mesh['y'=8,'z'=16,'p'=8] {'z'}, dimensions={0} | all-to-all | bytes 131072 | tf_op jit(solution)/shard_map/all_to_all | solution.py:22
  146.8 0.7 shard_map.43
  147.5 10.5 %all_to_all.60.parts = f32[8,8,256]{2,1,0:T(8,128)S(1)} all-to-all(f32[8,8,256]{2,1,0:T(8,128)S(1)} %get-tuple-element.22), channel_id=1, replica_groups=mesh['y'=8,'z'=16,'p'=8] {'p'}, dimensions={0} | all-to-all | bytes 131072 | tf_op jit(solution)/shard_map/all_to_all | solution.py:22
  158.0 9.7 %all_to_all.61.parts = f32[8,8,256]{2,1,0:T(8,128)S(1)} all-to-all(f32[8,8,256]{2,1,0:T(8,128)S(1)} %shard_map.44), channel_id=1, replica_groups=mesh['y'=8,'z'=16,'p'=8] {'y'}, dimensions={0} | all-to-all | bytes 131072 | tf_op jit(solution)/shard_map/all_to_all | solution.py:22
  168.4 14.2 %all_to_all.62.parts = f32[16,1,1024]{2,1,0:T(1,128)S(1)} all-to-all(f32[16,1,1024]{2,1,0:T(1,128)S(1)} %shard_map.45), channel_id=1, replica_groups=mesh['y'=8,'z'=16,'p'=8] {'z'}, dimensions={0} | all-to-all | bytes 131072 | tf_op jit(solution)/shard_map/all_to_all | solution.py:22
  183.2 10.4 %all_to_all.63.parts = f32[8,8,256]{2,1,0:T(8,128)S(1)} all-to-all(f32[8,8,256]{2,1,0:T(8,128)S(1)} %get-tuple-element.23), channel_id=1, replica_groups=mesh['y'=8,'z'=16,'p'=8] {'p'}, dimensions={0} | all-to-all | bytes 131072 | tf_op jit(solution)/shard_map/all_to_all | solution.py:22
  193.6 9.6 %all_to_all.64.got = f32[8,1,1280]{2,1,0:T(1,128)S(1)} all-to-all(f32[8,1,1280]{2,1,0:T(1,128)S(1)} %shard_map.47), channel_id=1, replica_groups=mesh['y'=8,'z'=16,'p'=8] {'y'}, dimensions={0} | all-to-all | bytes 81920 | tf_op jit(solution)/shard_map/all_to_all | solution.py:22
  203.2 3.9 %shard_map.48 = bf16[192,8192]{1,0:T(8,128)(2,1)} custom-call(bf16[192,256]{1,0:T(8,128)(2,1)S(1)} %get-tuple-element.15.mine, f32[192,128]{1,0:T(8,128)S(1)} %get-tuple-element.16.mine_scale, bf16[8,256,1024]{2,1,0:T(8,128)(2,1)S(1)} %copy-done, f32[8,1,1280]{2,1,0:T(1,128)S(1)} %all_to_all.64.got), custom_call_target="tpu_custom_call" | custom-call | flops 805306368 | bytes 9437184 | tf_op jit(solution)/shard_map/pallas_call | solution.py:275
  (20 shorter events, 2.1 us)
Async XLA Ops:
  24.1 40.2 %all-to-all-start.1 = ((bf16[16,16,1024]{2,1,0:T(8,128)(2,1)}), bf16[16,16,1024]{2,1,0:T(8,128)(2,1)S(1)}, u32[]{:S(2)}, u32[]{:S(2)}) async-start(bf16[16,16,1024]{2,1,0:T(8,128)(2,1)} %broadcast_in_dim.3), calls=%async_computation.1 | async-start | bytes 1048576 | tf_op jit(solution)/shard_map/all_to_all | solution.py:22
  42.6 35.6 %all-gather.6.cloned.1.call-start = ((), (), s32[]{:S(2)}) async-start(), calls=%async_computation.12 | async-start | bytes 1179648 | tf_op jit(solution)/shard_map/all_gather | solution.py:225
  43.4 150.1 %all-gather.4.cloned.1.call-start = ((), (), s32[]{:S(2)}) async-start(), calls=%async_computation.11 | async-start | bytes 4718592 | tf_op jit(solution)/shard_map/all_gather | solution.py:240
  64.3 0.8 copy-start.1
  78.3 1.2 copy-start.3
  80.3 1.0 copy-start.2
  193.5 9.6 %copy-start = (bf16[8,256,1024]{2,1,0:T(8,128)(2,1)S(1)}, bf16[8,256,1024]{2,1,0:T(8,128)(2,1)}, u32[]{:S(2)}) copy-start(bf16[8,256,1024]{2,1,0:T(8,128)(2,1)} %all-gather.4.cloned.1.call-done.every_proto.protos) | copy-start | bytes 12582916
Sparse Core Ops, SparseCore 0:
  46.2 32.0 all-gather.5
  80.9 63.3 all-gather.3

commit v6 on v5

--- a/solution.py
+++ b/solution.py
@@ -20,11 +20,6 @@
 
 def exchange(value, axes):
     return lax.all_to_all(value, axes, split_axis=0, concat_axis=0, tiled=True)
-
-
-def from_everyone(value, axes):
-    copies = jnp.broadcast_to(value, (lax.axis_size(axes), *value.shape))
-    return exchange(copies, axes)
 
 
 def in_hbm(value):
@@ -64,6 +59,24 @@
         both[y, held:, :] = chosen
 
 
+def second_body(both, chosen, pieces):
+    ny = both.shape[0]
+    nz, _, _ = pieces.shape
+    lanes = both.shape[2]
+    held = both.shape[1] - chosen.shape[1]
+    chosen[...] = both[:, held:, :]
+    for y in range(ny):
+        for at in range(0, held, 2):
+            pair = both[y, at : at + 2, :]
+            start = at // 2 * lanes
+            for z in range(nz):
+                pieces[z, 2 * y : 2 * y + 2, start : start + lanes] = pair
+
+
+def keep_body(protos, kept):
+    kept[...] = protos[...]
+
+
 def squared_scale(protos):
     wide = protos.astype(jnp.float32)
     return lax.rsqrt(jnp.sum(wide * wide, axis=0, keepdims=True) + EPS)
@@ -91,18 +104,23 @@
     return hit.astype(jnp.float32).astype(jnp.bfloat16)
 
 
-def feats_body(nz, me, patches, feats, scales, mine, mine_scale):
-    npr, ny, share, lanes = patches.shape
+def feats_body(nz, ny, me, patches, feats, scales, mine, mine_scale):
+    npr, count, share, lanes = patches.shape
     n = feats.shape[1]
+    step = pl.program_id(0)
     order = arrival_order(ny, nz)
-    for y in range(ny):
-        feat = patches[:, y].reshape(npr * share, lanes)
+    for k in range(count):
+        y = step * count + k
+        feat = patches[:, k].reshape(npr * share, lanes)
         scales[y] = jnp.broadcast_to(squared_scale(feat), (LANES, lanes)).T[:n]
         feats[y] = lax.dot_general(
             feat.T[:n], order, (((1,), (0,)), ((), ())), preferred_element_type=jnp.float32
         ).astype(jnp.bfloat16)
-    mine[...] = feats[me[0]]
-    mine_scale[...] = scales[me[0]]
+
+    @pl.when(step == pl.num_programs(0) - 1)
+    def _():
+        mine[...] = feats[me[0]]
+        mine_scale[...] = scales[me[0]]
 
 
 def weights_body(feats, scales, protos, weights, col_part):
@@ -220,12 +238,24 @@
         out_specs=VMEM,
     )(in_hbm(features.T), in_hbm(prototypes.T), in_hbm(masked_index.reshape(1, n)))
     both = exchange(both, "y")
-    pieces = both[:, :held].reshape(ny, held // 2, 2, lanes).transpose(0, 2, 1, 3)
-    pieces = pieces.reshape(2 * ny, k_own)
-    patches = lax.all_gather(both[:, held:], "p")
-    protos = from_everyone(pieces, "z").reshape(dim, k_own)
+    chosen, pieces = call(
+        second_body,
+        (
+            jax.ShapeDtypeStruct((ny, share, lanes), bf16),
+            jax.ShapeDtypeStruct((nz, 2 * ny, k_own), bf16),
+        ),
+        ny * share * lanes, 4 * dim * k_own,
+        grid=(1,),
+        in_specs=[VMEM],
+        out_specs=(
+            pl.BlockSpec((ny, share, lanes), lambda i: (0, 0, 0)),
+            pl.BlockSpec((nz, 2 * ny, k_own), lambda i: (0, 0, 0)),
+        ),
+    )(both)
+    patches = lax.all_gather(chosen, "p")
+    protos = exchange(pieces, "z").reshape(dim, k_own)
     prepared = call(
-        functools.partial(feats_body, nz),
+        functools.partial(feats_body, nz, ny),
         (
             jax.ShapeDtypeStruct((ny, n, dim), bf16),
             jax.ShapeDtypeStruct((ny, n, LANES), f32),
@@ -233,11 +263,21 @@
             jax.ShapeDtypeStruct((n, LANES), f32),
         ),
         2 * ny * lanes * dim, 4 * ny * lanes * dim,
-        in_specs=[pl.BlockSpec(memory_space=pltpu.SMEM), VMEM],
+        grid=(2,),
+        in_specs=[
+            pl.BlockSpec(memory_space=pltpu.SMEM),
+            pl.BlockSpec((npr, ny // 2, share, lanes), lambda i: (0, i, 0, 0)),
+        ],
         out_specs=(VMEM, VMEM, VMEM, VMEM),
-    )(lax.axis_index("y").reshape(1), patches)
+    )(lax.axis_index("y").reshape(1), in_hbm(patches))
     feats, scales, mine, mine_scale = prepared
-    every_proto = lax.all_gather(protos, "y")
+    kept = call(
+        keep_body, jax.ShapeDtypeStruct((dim, k_own), bf16), dim * k_own, 4 * dim * k_own,
+        grid=(1,),
+        in_specs=[VMEM],
+        out_specs=pl.BlockSpec((dim, k_own), lambda i: (0, 0)),
+    )(protos)
+    every_proto = lax.all_gather(kept, "y")
     weights, col_part = call(
         weights_body,
         (

time: 215 us -> 213 us (level)
  local copies, waits for them, and re-layouts: 4.65 us -> 0.01 us
  Pallas kernels: 10.5 us -> 13.5 us
    unnamed x9 -> x2, local copies, waits for them, and re-layouts: 3.06 us -> 0.01 us
    pallas_call x1 -> x3, Pallas kernels: 0.79 us -> 3.78 us  [the longest x1 1.94 us: on_device(): call(functools.partial(feats_body, nz, ny), (jax.ShapeDtypeStruct((ny, n,...]
  transfers between devices with their start and end apart: 3 -> 3, of which waited for: 2 -> 2; matrix products, arithmetic and copies ran while one was open for 0% -> 0% of each run, Pallas kernels for 3% -> 4%
where the time goes in v6:
time: 213 us
  blocking collectives  133 us (62%)
  waiting for transfers between devices  34.7 us (16%)
  starting transfers between devices  18.6 us (9%)
  Pallas kernels  13.5 us (6%)
  between operations  13.5 us (6%)
    all_to_all x10, blocking collectives, exchange(): return lax.all_to_all(value, axes, split_axis=0, concat_axis=0, tiled=True)  133 us
    all_to_all x1, waiting for transfers between devices, exchange(): return lax.all_to_all(value, axes, split_axis=0, concat_axis=0, tiled=True)  20.9 us
    all_to_all x1, starting transfers between devices, exchange(): return lax.all_to_all(value, axes, split_axis=0, concat_axis=0, tiled=True)  18.5 us
    all_gather x1, waiting for transfers between devices, on_device(): patches = lax.all_gather(chosen, 'p')  13.1 us
  transfers between devices with their start and end apart: 3, of which 2 were waited for; matrix products, arithmetic and copies ran while one was open for 0% of the time, Pallas kernels for 4%

profile of v6, /device:TPU:1, one launch (start us, length us, event | category | flops | bytes accessed | tf_op | source)
XLA Modules:
  0.0 212.8 jit_solution(3636776260768641854)
XLA Ops:
  6.5 0.9 shard_map.37
  7.5 15.7 %all_to_all.55.both = bf16[8,40,256]{2,1,0:T(8,128)(2,1)S(1)} all-to-all(bf16[8,40,256]{2,1,0:T(8,128)(2,1)S(1)} %shard_map.37), channel_id=1, replica_groups=mesh['y'=8,'z'=16,'p'=8] {'y'}, dimensions={0} | all-to-all | bytes 327680 | tf_op jit(solution)/shard_map/all_to_all | solution.py:22
  23.2 1.0 shard_map.38
  24.2 18.5 %all-to-all-start.1 = ((bf16[16,16,1024]{2,1,0:T(8,128)(2,1)}), bf16[16,16,1024]{2,1,0:T(8,128)(2,1)S(1)}, u32[]{:S(2)}, u32[]{:S(2)}) async-start(bf16[16,16,1024]{2,1,0:T(8,128)(2,1)} %get-tuple-element.20), calls=%async_computation.1 | async-start | bytes 1048576 | tf_op jit(solution)/shard_map/all_to_all | solution.py:22
  42.8 0.7 all-gather.5.cloned.1.call-update
  43.5 20.9 %all-to-all-done.1 = bf16[16,16,1024]{2,1,0:T(8,128)(2,1)S(1)} async-done(((bf16[16,16,1024]{2,1,0:T(8,128)(2,1)}), bf16[16,16,1024]{2,1,0:T(8,128)(2,1)S(1)}, u32[]{:S(2)}, u32[]{:S(2)}) %all-to-all-start.1) | async-done | bytes 524320 | tf_op jit(solution)/shard_map/all_to_all | solution.py:22
  64.4 0.8 shard_map.40
  65.3 13.1 %all-gather.5.cloned.1.call-done = bf16[64,32,256]{2,1,0:T(8,128)(2,1)} async-done(((bf16[8,32,256]{2,1,0:T(8,128)(2,1)}), bf16[64,32,256]{2,1,0:T(8,128)(2,1)}) %all-gather.5.cloned.1.call-update) | async-done | bytes 1048592 | tf_op jit(solution)/shard_map/all_gather | solution.py:255
  78.4 1.9 shard_map.39
  80.3 1.6 shard_map.41
  81.9 24.1 %all_to_all.56.parts = f32[16,1,1024]{2,1,0:T(1,128)S(1)} all-to-all(f32[16,1,1024]{2,1,0:T(1,128)S(1)} %get-tuple-element.24), channel_id=1, replica_groups=mesh['y'=8,'z'=16,'p'=8] {'z'}, dimensions={0} | all-to-all | bytes 131072 | tf_op jit(solution)/shard_map/all_to_all | solution.py:22
  106.1 0.7 shard_map.42
  106.8 9.7 %all_to_all.57.parts = f32[8,8,256]{2,1,0:T(8,128)S(1)} all-to-all(f32[8,8,256]{2,1,0:T(8,128)S(1)} %get-tuple-element.25), channel_id=1, replica_groups=mesh['y'=8,'z'=16,'p'=8] {'p'}, dimensions={0} | all-to-all | bytes 131072 | tf_op jit(solution)/shard_map/all_to_all | solution.py:22
  116.5 14.4 %all_to_all.58.parts = f32[8,8,256]{2,1,0:T(8,128)S(1)} all-to-all(f32[8,8,256]{2,1,0:T(8,128)S(1)} %shard_map.43), channel_id=1, replica_groups=mesh['y'=8,'z'=16,'p'=8] {'y'}, dimensions={0} | all-to-all | bytes 131072 | tf_op jit(solution)/shard_map/all_to_all | solution.py:22
  130.8 0.7 shard_map.44
  131.5 14.2 %all_to_all.59.parts = f32[16,1,1024]{2,1,0:T(1,128)S(1)} all-to-all(f32[16,1,1024]{2,1,0:T(1,128)S(1)} %shard_map.44), channel_id=1, replica_groups=mesh['y'=8,'z'=16,'p'=8] {'z'}, dimensions={0} | all-to-all | bytes 131072 | tf_op jit(solution)/shard_map/all_to_all | solution.py:22
  145.7 0.7 shard_map.45
  146.4 10.5 %all_to_all.60.parts = f32[8,8,256]{2,1,0:T(8,128)S(1)} all-to-all(f32[8,8,256]{2,1,0:T(8,128)S(1)} %get-tuple-element.26), channel_id=1, replica_groups=mesh['y'=8,'z'=16,'p'=8] {'p'}, dimensions={0} | all-to-all | bytes 131072 | tf_op jit(solution)/shard_map/all_to_all | solution.py:22
  157.0 9.7 %all_to_all.61.parts = f32[8,8,256]{2,1,0:T(8,128)S(1)} all-to-all(f32[8,8,256]{2,1,0:T(8,128)S(1)} %shard_map.46), channel_id=1, replica_groups=mesh['y'=8,'z'=16,'p'=8] {'y'}, dimensions={0} | all-to-all | bytes 131072 | tf_op jit(solution)/shard_map/all_to_all | solution.py:22
  166.7 0.7 shard_map.47
  167.3 14.2 %all_to_all.62.parts = f32[16,1,1024]{2,1,0:T(1,128)S(1)} all-to-all(f32[16,1,1024]{2,1,0:T(1,128)S(1)} %shard_map.47), channel_id=1, replica_groups=mesh['y'=8,'z'=16,'p'=8] {'z'}, dimensions={0} | all-to-all | bytes 131072 | tf_op jit(solution)/shard_map/all_to_all | solution.py:22
  182.1 10.4 %all_to_all.63.parts = f32[8,8,256]{2,1,0:T(8,128)S(1)} all-to-all(f32[8,8,256]{2,1,0:T(8,128)S(1)} %get-tuple-element.27), channel_id=1, replica_groups=mesh['y'=8,'z'=16,'p'=8] {'p'}, dimensions={0} | all-to-all | bytes 131072 | tf_op jit(solution)/shard_map/all_to_all | solution.py:22
  192.5 9.6 %all_to_all.64.got = f32[8,1,1280]{2,1,0:T(1,128)S(1)} all-to-all(f32[8,1,1280]{2,1,0:T(1,128)S(1)} %shard_map.49), channel_id=1, replica_groups=mesh['y'=8,'z'=16,'p'=8] {'y'}, dimensions={0} | all-to-all | bytes 81920 | tf_op jit(solution)/shard_map/all_to_all | solution.py:22
  202.1 3.9 %shard_map.50 = bf16[192,8192]{1,0:T(8,128)(2,1)} custom-call(bf16[192,256]{1,0:T(8,128)(2,1)S(1)} %get-tuple-element.18.mine, f32[192,128]{1,0:T(8,128)S(1)} %get-tuple-element.19.mine_scale, bf16[8,256,1024]{2,1,0:T(8,128)(2,1)S(1)} %bitcast.8, f32[8,1,1280]{2,1,0:T(1,128)S(1)} %all_to_all.64.got), custom_call_target="tpu_custom_call" | custom-call | flops 805306368 | bytes 9437184 | tf_op jit(solution)/shard_map/pallas_call | solution.py:315
  (10 shorter events, 0.7 us)
Async XLA Ops:
  24.2 40.2 %all-to-all-start.1 = ((bf16[16,16,1024]{2,1,0:T(8,128)(2,1)}), bf16[16,16,1024]{2,1,0:T(8,128)(2,1)S(1)}, u32[]{:S(2)}, u32[]{:S(2)}) async-start(bf16[16,16,1024]{2,1,0:T(8,128)(2,1)} %get-tuple-element.20), calls=%async_computation.1 | async-start | bytes 1048576 | tf_op jit(solution)/shard_map/all_to_all | solution.py:22
  42.7 35.6 %all-gather.5.cloned.1.call-start = ((), (), s32[]{:S(2)}) async-start(), calls=%async_computation.11 | async-start | bytes 1179648 | tf_op jit(solution)/shard_map/all_gather | solution.py:255
  43.5 149.0 %all-gather.7.cloned.1.call-start = ((), (), s32[]{:S(2)}) async-start(), calls=%async_computation.12 | async-start | bytes 4718592 | tf_op jit(solution)/shard_map/all_gather | solution.py:280
  192.5 9.6 %copy-start = (bf16[2048,1024]{1,0:T(8,128)(2,1)S(1)}, bf16[2048,1024]{1,0:T(8,128)(2,1)}, u32[]{:S(2)}) copy-start(bf16[2048,1024]{1,0:T(8,128)(2,1)} %all-gather.7.cloned.1.call-done) | copy-start | bytes 12582916
Sparse Core Ops, SparseCore 0:
  46.3 32.0 all-gather.4
  81.0 63.3 all-gather.6

commit v7 on v6

--- a/solution.py
+++ b/solution.py
@@ -73,8 +73,10 @@
                 pieces[z, 2 * y : 2 * y + 2, start : start + lanes] = pair
 
 
-def keep_body(protos, kept):
-    kept[...] = protos[...]
+def keep_body(protos, kept, sem):
+    copy = pltpu.make_async_copy(protos, kept, sem)
+    copy.start()
+    copy.wait()
 
 
 def squared_scale(protos):
@@ -188,29 +190,29 @@
         sent[y, :, lanes:] = col_scale[...]
 
 
-def targets_body(total_rows, mine, mine_scale, protos, got, out, row_scale):
-    step = pl.program_id(0)
-    n = out.shape[0]
-    width = protos.shape[2]
+def targets_body(total_rows, mine, mine_scale, protos, got, out, slots, sems):
+    count, n, width = slots.shape
     lanes = got.shape[2] - width
-
-    @pl.when(step == 0)
-    def _():
-        total = got[0, :, :lanes]
-        for k in range(1, got.shape[0]):
-            total = total + got[k, :, :lanes]
-        factor = float(K) * float(total_rows)
-        scale = factor * (1.0 / (total_rows * total))
-        row_scale[...] = jnp.broadcast_to(scale, (LANES, lanes)).T[:n]
-
-    count = out.shape[1] // width
-    for k in range(count):
-        y = step * count + k
+    total = got[0, :, :lanes]
+    for k in range(1, got.shape[0]):
+        total = total + got[k, :, :lanes]
+    factor = float(K) * float(total_rows)
+    scale = factor * (1.0 / (total_rows * total))
+    scale = jnp.broadcast_to(scale, (LANES, lanes)).T[:n]
+    copies = []
+    for y in range(count):
         block = block_weights(mine[...], mine_scale[...], protos[y])
         col_scale = got[y][:, lanes:]
         for at in range(0, width, LANES):
-            part = row_scale[...] * block[:, at : at + LANES] * col_scale[:, at : at + LANES]
-            out[:, k * width + at : k * width + at + LANES] = part.astype(jnp.bfloat16)
+            part = scale * block[:, at : at + LANES] * col_scale[:, at : at + LANES]
+            slots[y, :, at : at + LANES] = part.astype(jnp.bfloat16)
+        copy = pltpu.make_async_copy(
+            slots.at[y], out.at[:, y * width : (y + 1) * width], sems.at[y]
+        )
+        copy.start()
+        copies.append(copy)
+    for copy in copies:
+        copy.wait()
 
 
 def on_device(features, prototypes, masked_index):
@@ -273,9 +275,9 @@
     feats, scales, mine, mine_scale = prepared
     kept = call(
         keep_body, jax.ShapeDtypeStruct((dim, k_own), bf16), dim * k_own, 4 * dim * k_own,
-        grid=(1,),
         in_specs=[VMEM],
-        out_specs=pl.BlockSpec((dim, k_own), lambda i: (0, 0)),
+        out_specs=pl.BlockSpec(memory_space=pltpu.HBM),
+        scratch_shapes=[pltpu.SemaphoreType.DMA],
     )(protos)
     every_proto = lax.all_gather(kept, "y")
     weights, col_part = call(
@@ -316,10 +318,9 @@
         functools.partial(targets_body, total_rows),
         jax.ShapeDtypeStruct((n, k_out), bf16),
         2 * elements * dim, 6 * elements,
-        grid=(ny // 2,),
         in_specs=[VMEM, VMEM, VMEM, VMEM],
-        out_specs=pl.BlockSpec((n, 2 * k_own), lambda i: (0, i)),
-        scratch_shapes=[pltpu.VMEM((n, LANES), f32)],
+        out_specs=pl.BlockSpec(memory_space=pltpu.HBM),
+        scratch_shapes=[pltpu.VMEM((ny, n, k_own), bf16), pltpu.SemaphoreType.DMA((ny,))],
     )(mine, mine_scale, every_proto, exchange(sent, "y"))
 
 

time: 213 us -> 213 us (level)
  no operation moved by 1% of the time
where the time goes in v7:
time: 213 us; the launch traced here: 212 us
  blocking collectives  133 us (62%)
  waiting for transfers between devices  34.7 us (16%)
  starting transfers between devices  18.6 us (9%)
  between operations  13.5 us (6%)
  Pallas kernels  13 us (6%)
    all_to_all x10, blocking collectives, exchange(): return lax.all_to_all(value, axes, split_axis=0, concat_axis=0, tiled=True)  133 us
    all_to_all x1, waiting for transfers between devices, exchange(): return lax.all_to_all(value, axes, split_axis=0, concat_axis=0, tiled=True)  20.9 us
    all_to_all x1, starting transfers between devices, exchange(): return lax.all_to_all(value, axes, split_axis=0, concat_axis=0, tiled=True)  18.5 us
    all_gather x1, waiting for transfers between devices, on_device(): patches = lax.all_gather(chosen, 'p')  13.1 us
  transfers between devices with their start and end apart: 3, of which 2 were waited for; matrix products, arithmetic and copies ran while one was open for 0% of the time, Pallas kernels for 4%

profile of v7, /device:TPU:1, one launch (start us, length us, event | category | flops | bytes accessed | tf_op | source)
XLA Modules:
  0.0 212.4 jit_solution(4477675718412188325)
XLA Ops:
  6.5 0.9 shard_map.37
  7.5 15.7 %all_to_all.55.both = bf16[8,40,256]{2,1,0:T(8,128)(2,1)S(1)} all-to-all(bf16[8,40,256]{2,1,0:T(8,128)(2,1)S(1)} %shard_map.37), channel_id=1, replica_groups=mesh['y'=8,'z'=16,'p'=8] {'y'}, dimensions={0} | all-to-all | bytes 327680 | tf_op jit(solution)/shard_map/all_to_all | solution.py:22
  23.2 1.0 shard_map.38
  24.2 18.5 %all-to-all-start.1 = ((bf16[16,16,1024]{2,1,0:T(8,128)(2,1)}), bf16[16,16,1024]{2,1,0:T(8,128)(2,1)S(1)}, u32[]{:S(2)}, u32[]{:S(2)}) async-start(bf16[16,16,1024]{2,1,0:T(8,128)(2,1)} %get-tuple-element.20), calls=%async_computation.1 | async-start | bytes 1048576 | tf_op jit(solution)/shard_map/all_to_all | solution.py:22
  42.8 0.7 all-gather.5.cloned.1.call-update
  43.5 20.9 %all-to-all-done.1 = bf16[16,16,1024]{2,1,0:T(8,128)(2,1)S(1)} async-done(((bf16[16,16,1024]{2,1,0:T(8,128)(2,1)}), bf16[16,16,1024]{2,1,0:T(8,128)(2,1)S(1)}, u32[]{:S(2)}, u32[]{:S(2)}) %all-to-all-start.1) | async-done | bytes 524320 | tf_op jit(solution)/shard_map/all_to_all | solution.py:22
  64.4 0.8 shard_map.40
  65.3 13.1 %all-gather.5.cloned.1.call-done = bf16[64,32,256]{2,1,0:T(8,128)(2,1)} async-done(((bf16[8,32,256]{2,1,0:T(8,128)(2,1)}), bf16[64,32,256]{2,1,0:T(8,128)(2,1)}) %all-gather.5.cloned.1.call-update) | async-done | bytes 1048592 | tf_op jit(solution)/shard_map/all_gather | solution.py:257
  78.4 1.9 shard_map.39
  80.3 1.6 shard_map.41
  81.9 24.1 %all_to_all.56.parts = f32[16,1,1024]{2,1,0:T(1,128)S(1)} all-to-all(f32[16,1,1024]{2,1,0:T(1,128)S(1)} %get-tuple-element.24), channel_id=1, replica_groups=mesh['y'=8,'z'=16,'p'=8] {'z'}, dimensions={0} | all-to-all | bytes 131072 | tf_op jit(solution)/shard_map/all_to_all | solution.py:22
  106.1 0.7 shard_map.42
  106.8 9.7 %all_to_all.57.parts = f32[8,8,256]{2,1,0:T(8,128)S(1)} all-to-all(f32[8,8,256]{2,1,0:T(8,128)S(1)} %get-tuple-element.25), channel_id=1, replica_groups=mesh['y'=8,'z'=16,'p'=8] {'p'}, dimensions={0} | all-to-all | bytes 131072 | tf_op jit(solution)/shard_map/all_to_all | solution.py:22
  116.5 14.4 %all_to_all.58.parts = f32[8,8,256]{2,1,0:T(8,128)S(1)} all-to-all(f32[8,8,256]{2,1,0:T(8,128)S(1)} %shard_map.43), channel_id=1, replica_groups=mesh['y'=8,'z'=16,'p'=8] {'y'}, dimensions={0} | all-to-all | bytes 131072 | tf_op jit(solution)/shard_map/all_to_all | solution.py:22
  130.8 0.7 shard_map.44
  131.5 14.2 %all_to_all.59.parts = f32[16,1,1024]{2,1,0:T(1,128)S(1)} all-to-all(f32[16,1,1024]{2,1,0:T(1,128)S(1)} %shard_map.44), channel_id=1, replica_groups=mesh['y'=8,'z'=16,'p'=8] {'z'}, dimensions={0} | all-to-all | bytes 131072 | tf_op jit(solution)/shard_map/all_to_all | solution.py:22
  145.7 0.7 shard_map.45
  146.4 10.5 %all_to_all.60.parts = f32[8,8,256]{2,1,0:T(8,128)S(1)} all-to-all(f32[8,8,256]{2,1,0:T(8,128)S(1)} %get-tuple-element.26), channel_id=1, replica_groups=mesh['y'=8,'z'=16,'p'=8] {'p'}, dimensions={0} | all-to-all | bytes 131072 | tf_op jit(solution)/shard_map/all_to_all | solution.py:22
  157.0 9.7 %all_to_all.61.parts = f32[8,8,256]{2,1,0:T(8,128)S(1)} all-to-all(f32[8,8,256]{2,1,0:T(8,128)S(1)} %shard_map.46), channel_id=1, replica_groups=mesh['y'=8,'z'=16,'p'=8] {'y'}, dimensions={0} | all-to-all | bytes 131072 | tf_op jit(solution)/shard_map/all_to_all | solution.py:22
  166.7 0.7 shard_map.47
  167.3 14.2 %all_to_all.62.parts = f32[16,1,1024]{2,1,0:T(1,128)S(1)} all-to-all(f32[16,1,1024]{2,1,0:T(1,128)S(1)} %shard_map.47), channel_id=1, replica_groups=mesh['y'=8,'z'=16,'p'=8] {'z'}, dimensions={0} | all-to-all | bytes 131072 | tf_op jit(solution)/shard_map/all_to_all | solution.py:22
  182.1 10.4 %all_to_all.63.parts = f32[8,8,256]{2,1,0:T(8,128)S(1)} all-to-all(f32[8,8,256]{2,1,0:T(8,128)S(1)} %get-tuple-element.27), channel_id=1, replica_groups=mesh['y'=8,'z'=16,'p'=8] {'p'}, dimensions={0} | all-to-all | bytes 131072 | tf_op jit(solution)/shard_map/all_to_all | solution.py:22
  192.5 9.6 %all_to_all.64.got = f32[8,1,1280]{2,1,0:T(1,128)S(1)} all-to-all(f32[8,1,1280]{2,1,0:T(1,128)S(1)} %shard_map.49), channel_id=1, replica_groups=mesh['y'=8,'z'=16,'p'=8] {'y'}, dimensions={0} | all-to-all | bytes 81920 | tf_op jit(solution)/shard_map/all_to_all | solution.py:22
  202.1 3.4 %shard_map.50 = bf16[192,8192]{1,0:T(8,128)(2,1)} custom-call(bf16[192,256]{1,0:T(8,128)(2,1)S(1)} %get-tuple-element.18.mine, f32[192,128]{1,0:T(8,128)S(1)} %get-tuple-element.19.mine_scale, bf16[8,256,1024]{2,1,0:T(8,128)(2,1)S(1)} %bitcast.8, f32[8,1,1280]{2,1,0:T(1,128)S(1)} %all_to_all.64.got), custom_call_target="tpu_custom_call" | custom-call | flops 805306368 | bytes 9437184 | tf_op jit(solution)/shard_map/pallas_call | solution.py:317
  (10 shorter events, 0.7 us)
Async XLA Ops:
  24.2 40.2 %all-to-all-start.1 = ((bf16[16,16,1024]{2,1,0:T(8,128)(2,1)}), bf16[16,16,1024]{2,1,0:T(8,128)(2,1)S(1)}, u32[]{:S(2)}, u32[]{:S(2)}) async-start(bf16[16,16,1024]{2,1,0:T(8,128)(2,1)} %get-tuple-element.20), calls=%async_computation.1 | async-start | bytes 1048576 | tf_op jit(solution)/shard_map/all_to_all | solution.py:22
  42.7 35.6 %all-gather.5.cloned.1.call-start = ((), (), s32[]{:S(2)}) async-start(), calls=%async_computation.11 | async-start | bytes 1179648 | tf_op jit(solution)/shard_map/all_gather | solution.py:257
  43.5 149.0 %all-gather.7.cloned.1.call-start = ((), (), s32[]{:S(2)}) async-start(), calls=%async_computation.12 | async-start | bytes 4718592 | tf_op jit(solution)/shard_map/all_gather | solution.py:282
  192.5 9.6 %copy-start = (bf16[2048,1024]{1,0:T(8,128)(2,1)S(1)}, bf16[2048,1024]{1,0:T(8,128)(2,1)}, u32[]{:S(2)}) copy-start(bf16[2048,1024]{1,0:T(8,128)(2,1)} %all-gather.7.cloned.1.call-done) | copy-start | bytes 12582916
Sparse Core Ops, SparseCore 0:
  46.3 32.0 all-gather.4
  81.0 63.3 all-gather.6

commit v8 on v7

--- a/solution.py
+++ b/solution.py
@@ -14,6 +14,7 @@
 TEMP = 0.07
 EPS = 1e-06
 NY = 8
+CORES = 2
 LANES = 128
 VMEM = pl.BlockSpec(memory_space=pltpu.VMEM)
 
@@ -125,7 +126,7 @@
         mine_scale[...] = scales[me[0]]
 
 
-def weights_body(feats, scales, protos, weights, col_part):
+def weights_body(core, feats, scales, protos, weights, col_part):
     values = protos[...]
     total = jnp.zeros((8, values.shape[1]), jnp.float32)
     for y in range(feats.shape[0]):
@@ -182,15 +183,17 @@
         copies[y] = total
 
 
-def last_body(parts, col_scale, every_proto, sent):
+def last_body(core, parts, col_scale, every_proto, sent):
     total = added(parts)
     lanes = total.shape[1]
-    for y in range(sent.shape[0]):
-        sent[y, :, :lanes] = total[y : y + 1]
-        sent[y, :, lanes:] = col_scale[...]
-
-
-def targets_body(total_rows, mine, mine_scale, protos, got, out, slots, sems):
+    pairs = sent.shape[0] // total.shape[0]
+    for k in range(sent.shape[0]):
+        y = k // pairs
+        sent[k, :, :lanes] = total[y : y + 1]
+        sent[k, :, lanes:] = col_scale[...]
+
+
+def targets_body(total_rows, core, mine, mine_scale, protos, got, out, slots, sems):
     count, n, width = slots.shape
     lanes = got.shape[2] - width
     total = got[0, :, :lanes]
@@ -202,7 +205,7 @@
     copies = []
     for y in range(count):
         block = block_weights(mine[...], mine_scale[...], protos[y])
-        col_scale = got[y][:, lanes:]
+        col_scale = got[y * (got.shape[0] // count) + core[0]][:, lanes:]
         for at in range(0, width, LANES):
             part = scale * block[:, at : at + LANES] * col_scale[:, at : at + LANES]
             slots[y, :, at : at + LANES] = part.astype(jnp.bfloat16)
@@ -217,7 +220,8 @@
 
 def on_device(features, prototypes, masked_index):
     n = masked_index.shape[0]
-    ny, nz, npr = lax.axis_size("y"), lax.axis_size("z"), lax.axis_size("p")
+    ny, nz, npr = lax.axis_size("y"), lax.axis_size("z"), lax.axis_size(("x", "c"))
+    nx, nc = lax.axis_size("x"), lax.axis_size("c")
     total_rows = n * ny * nz
     k_out = prototypes.shape[0]
     k_own = k_out // ny
@@ -254,7 +258,7 @@
             pl.BlockSpec((nz, 2 * ny, k_own), lambda i: (0, 0, 0)),
         ),
     )(both)
-    patches = lax.all_gather(chosen, "p")
+    patches = lax.all_gather(chosen, ("x", "c"))
     protos = exchange(pieces, "z").reshape(dim, k_own)
     prepared = call(
         functools.partial(feats_body, nz, ny),
@@ -272,6 +276,7 @@
         ],
         out_specs=(VMEM, VMEM, VMEM, VMEM),
     )(lax.axis_index("y").reshape(1), in_hbm(patches))
+    core = lax.axis_index("c").reshape(1)
     feats, scales, mine, mine_scale = prepared
     kept = call(
         keep_body, jax.ShapeDtypeStruct((dim, k_own), bf16), dim * k_own, 4 * dim * k_own,
@@ -287,21 +292,22 @@
             jax.ShapeDtypeStruct((nz, 1, k_own), f32),
         ),
         2 * elements * dim, 4 * elements,
-        in_specs=[VMEM, VMEM, VMEM], out_specs=(VMEM, VMEM),
-    )(feats, scales, protos)
+        in_specs=[pl.BlockSpec(memory_space=pltpu.SMEM), VMEM, VMEM, VMEM],
+        out_specs=(VMEM, VMEM),
+    )(core, feats, scales, protos)
 
     for step in range(ITERS):
         parts = exchange(col_part, "z")
         row_part, col_scale = call(
             row_body,
-            (jax.ShapeDtypeStruct((npr, ny, lanes), f32), jax.ShapeDtypeStruct((1, k_own), f32)),
+            (jax.ShapeDtypeStruct((nx, ny, lanes), f32), jax.ShapeDtypeStruct((1, k_own), f32)),
             2 * elements, 4 * elements,
             in_specs=[VMEM, VMEM], out_specs=(VMEM, VMEM),
         )(weights, parts)
-        parts = exchange(row_part, "p")
+        parts = exchange(row_part, "x")
         if step + 1 < ITERS:
             copies = call(
-                relay_body, jax.ShapeDtypeStruct((ny, ny, lanes), f32),
+                relay_body, jax.ShapeDtypeStruct((ny * nc, ny, lanes), f32),
                 ny * ny * lanes, 8 * ny * ny * lanes, in_specs=[VMEM], out_specs=VMEM,
             )(parts)
             col_part = call(
@@ -309,26 +315,28 @@
                 jax.ShapeDtypeStruct((nz, 1, k_own), f32),
                 2 * elements, 4 * elements,
                 in_specs=[VMEM, VMEM], out_specs=VMEM,
-            )(weights, exchange(copies, "y"))
+            )(weights, exchange(copies, ("y", "c")))
     sent = call(
-        last_body, jax.ShapeDtypeStruct((ny, 1, lanes + k_own), f32),
-        ny * ny * lanes, 8 * ny * ny * lanes, in_specs=[VMEM, VMEM, pl.BlockSpec(memory_space=pl.ANY)], out_specs=VMEM,
-    )(parts, col_scale, in_hbm(every_proto))
+        last_body, jax.ShapeDtypeStruct((ny * nc, 1, lanes + k_own), f32),
+        ny * ny * lanes, 8 * ny * ny * lanes, in_specs=[pl.BlockSpec(memory_space=pltpu.SMEM), VMEM, VMEM, pl.BlockSpec(memory_space=pl.ANY)],
+        out_specs=VMEM,
+    )(core, parts, col_scale, in_hbm(every_proto))
     return call(
         functools.partial(targets_body, total_rows),
         jax.ShapeDtypeStruct((n, k_out), bf16),
         2 * elements * dim, 6 * elements,
-        in_specs=[VMEM, VMEM, VMEM, VMEM],
+        in_specs=[pl.BlockSpec(memory_space=pltpu.SMEM), VMEM, VMEM, VMEM, VMEM],
         out_specs=pl.BlockSpec(memory_space=pltpu.HBM),
         scratch_shapes=[pltpu.VMEM((ny, n, k_own), bf16), pltpu.SemaphoreType.DMA((ny,))],
-    )(mine, mine_scale, every_proto, exchange(sent, "y"))
+    )(core, mine, mine_scale, every_proto, exchange(sent, ("y", "c")))
 
 
 def solution(mesh):
-    rows = mesh.shape["rows"]
-    split = Mesh(mesh.devices.reshape(NY, rows // NY, mesh.shape["protos"]), ("y", "z", "p"))
-    in_specs = (P(("y", "z"), "p"), P("p", ("y", "z")), P(("y", "z")))
-    out_specs = P(("y", "z"), "p")
+    rows, protos = mesh.shape["rows"], mesh.shape["protos"]
+    split = Mesh(
+        mesh.devices.reshape(NY, rows // NY, protos // CORES, CORES), ("y", "z", "x", "c"))
+    in_specs = (P(("y", "z"), ("x", "c")), P(("x", "c"), ("y", "z")), P(("y", "z")))
+    out_specs = P(("y", "z"), ("x", "c"))
     return jax.shard_map(
         on_device, mesh=split, in_specs=in_specs, out_specs=out_specs, check_vma=False
     )

time: 213 us -> 218 us (1.023)
  blocking collectives: 133 us -> 137 us
    all_to_all x10, blocking collectives: 133 us -> 137 us  [exchange(): return lax.all_to_all(value, axes, split_axis=0, concat_axis=0, tiled=True)]
where the time goes in v8:
time: 218 us; the launch traced here: 217 us
  blocking collectives  137 us (63%)
  waiting for transfers between devices  34.7 us (16%)
  starting transfers between devices  18.6 us (9%)
  between operations  13.5 us (6%)
  Pallas kernels  13.3 us (6%)
    all_to_all x10, blocking collectives, exchange(): return lax.all_to_all(value, axes, split_axis=0, concat_axis=0, tiled=True)  137 us
    all_to_all x1, waiting for transfers between devices, exchange(): return lax.all_to_all(value, axes, split_axis=0, concat_axis=0, tiled=True)  20.9 us
    all_to_all x1, starting transfers between devices, exchange(): return lax.all_to_all(value, axes, split_axis=0, concat_axis=0, tiled=True)  18.5 us
    all_gather x1, waiting for transfers between devices, on_device(): patches = lax.all_gather(chosen, ('x', 'c'))  13.1 us
  transfers between devices with their start and end apart: 3, of which 2 were waited for; matrix products, arithmetic and copies ran while one was open for 0% of the time, Pallas kernels for 4%

profile of v8, /device:TPU:1, one launch (start us, length us, event | category | flops | bytes accessed | tf_op | source)
XLA Modules:
  0.0 217.4 jit_solution(9222013225935199471)
XLA Ops:
  6.5 0.9 shard_map.37
  7.5 15.7 %all_to_all.55.both = bf16[8,40,256]{2,1,0:T(8,128)(2,1)S(1)} all-to-all(bf16[8,40,256]{2,1,0:T(8,128)(2,1)S(1)} %shard_map.37), channel_id=1, replica_groups=mesh['y'=8,'z'=16,'x'=4,'c'=2] {'y'}, dimensions={0} | all-to-all | bytes 327680 | tf_op jit(solution)/shard_map/all_to_all | solution.py:23
  23.2 1.0 shard_map.38
  24.2 18.5 %all-to-all-start.1 = ((bf16[16,16,1024]{2,1,0:T(8,128)(2,1)}), bf16[16,16,1024]{2,1,0:T(8,128)(2,1)S(1)}, u32[]{:S(2)}, u32[]{:S(2)}) async-start(bf16[16,16,1024]{2,1,0:T(8,128)(2,1)} %get-tuple-element.20), calls=%async_computation.1 | async-start | bytes 1048576 | tf_op jit(solution)/shard_map/all_to_all | solution.py:23
  42.8 0.7 all-gather.5.cloned.1.call-update
  43.5 20.9 %all-to-all-done.1 = bf16[16,16,1024]{2,1,0:T(8,128)(2,1)S(1)} async-done(((bf16[16,16,1024]{2,1,0:T(8,128)(2,1)}), bf16[16,16,1024]{2,1,0:T(8,128)(2,1)S(1)}, u32[]{:S(2)}, u32[]{:S(2)}) %all-to-all-start.1) | async-done | bytes 524320 | tf_op jit(solution)/shard_map/all_to_all | solution.py:23
  64.4 0.8 shard_map.40
  65.3 13.1 %all-gather.5.cloned.1.call-done = bf16[64,32,256]{2,1,0:T(8,128)(2,1)} async-done(((bf16[8,32,256]{2,1,0:T(8,128)(2,1)}), bf16[64,32,256]{2,1,0:T(8,128)(2,1)}) %all-gather.5.cloned.1.call-update) | async-done | bytes 1048592 | tf_op jit(solution)/shard_map/all_gather | solution.py:261
  78.4 1.9 shard_map.39
  80.3 1.6 shard_map.41
  81.9 24.1 %all_to_all.56.parts = f32[16,1,1024]{2,1,0:T(1,128)S(1)} all-to-all(f32[16,1,1024]{2,1,0:T(1,128)S(1)} %get-tuple-element.24), channel_id=1, replica_groups=mesh['y'=8,'z'=16,'x'=4,'c'=2] {'z'}, dimensions={0} | all-to-all | bytes 131072 | tf_op jit(solution)/shard_map/all_to_all | solution.py:23
  106.1 0.7 shard_map.42
  106.8 6.7 %all_to_all.57.parts = f32[4,8,256]{2,1,0:T(8,128)S(1)} all-to-all(f32[4,8,256]{2,1,0:T(8,128)S(1)} %get-tuple-element.25), channel_id=1, replica_groups=mesh['y'=8,'z'=16,'x'=4,'c'=2] {'x'}, dimensions={0} | all-to-all | bytes 65536 | tf_op jit(solution)/shard_map/all_to_all | solution.py:23
  113.5 20.8 %all_to_all.58.parts = f32[16,8,256]{2,1,0:T(8,128)S(1)} all-to-all(f32[16,8,256]{2,1,0:T(8,128)S(1)} %shard_map.43), channel_id=1, replica_groups=mesh['y'=8,'z'=16,'x'=4,'c'=2] {'y','c'}, dimensions={0} | all-to-all | bytes 262144 | tf_op jit(solution)/shard_map/all_to_all | solution.py:23
  134.3 0.8 shard_map.44
  135.0 14.3 %all_to_all.59.parts = f32[16,1,1024]{2,1,0:T(1,128)S(1)} all-to-all(f32[16,1,1024]{2,1,0:T(1,128)S(1)} %shard_map.44), channel_id=1, replica_groups=mesh['y'=8,'z'=16,'x'=4,'c'=2] {'z'}, dimensions={0} | all-to-all | bytes 131072 | tf_op jit(solution)/shard_map/all_to_all | solution.py:23
  149.3 0.7 shard_map.45
  150.0 6.6 %all_to_all.60.parts = f32[4,8,256]{2,1,0:T(8,128)S(1)} all-to-all(f32[4,8,256]{2,1,0:T(8,128)S(1)} %get-tuple-element.26), channel_id=1, replica_groups=mesh['y'=8,'z'=16,'x'=4,'c'=2] {'x'}, dimensions={0} | all-to-all | bytes 65536 | tf_op jit(solution)/shard_map/all_to_all | solution.py:23
  156.6 14.6 %all_to_all.61.parts = f32[16,8,256]{2,1,0:T(8,128)S(1)} all-to-all(f32[16,8,256]{2,1,0:T(8,128)S(1)} %shard_map.46), channel_id=1, replica_groups=mesh['y'=8,'z'=16,'x'=4,'c'=2] {'y','c'}, dimensions={0} | all-to-all | bytes 262144 | tf_op jit(solution)/shard_map/all_to_all | solution.py:23
  171.3 0.8 shard_map.47
  172.1 14.4 %all_to_all.62.parts = f32[16,1,1024]{2,1,0:T(1,128)S(1)} all-to-all(f32[16,1,1024]{2,1,0:T(1,128)S(1)} %shard_map.47), channel_id=1, replica_groups=mesh['y'=8,'z'=16,'x'=4,'c'=2] {'z'}, dimensions={0} | all-to-all | bytes 131072 | tf_op jit(solution)/shard_map/all_to_all | solution.py:23
  186.9 6.7 %all_to_all.63.parts = f32[4,8,256]{2,1,0:T(8,128)S(1)} all-to-all(f32[4,8,256]{2,1,0:T(8,128)S(1)} %get-tuple-element.27), channel_id=1, replica_groups=mesh['y'=8,'z'=16,'x'=4,'c'=2] {'x'}, dimensions={0} | all-to-all | bytes 65536 | tf_op jit(solution)/shard_map/all_to_all | solution.py:23
  193.6 13.4 %all_to_all.64.got = f32[16,1,1280]{2,1,0:T(1,128)S(1)} all-to-all(f32[16,1,1280]{2,1,0:T(1,128)S(1)} %shard_map.49), channel_id=1, replica_groups=mesh['y'=8,'z'=16,'x'=4,'c'=2] {'y','c'}, dimensions={0} | all-to-all | bytes 163840 | tf_op jit(solution)/shard_map/all_to_all | solution.py:23
  207.0 3.5 %shard_map.50 = bf16[192,8192]{1,0:T(8,128)(2,1)} custom-call(s32[1]{0:T(128)} %bitcast.core, bf16[192,256]{1,0:T(8,128)(2,1)S(1)} %get-tuple-element.18.mine, f32[192,128]{1,0:T(8,128)S(1)} %get-tuple-element.19.mine_scale, bf16[8,256,1024]{2,1,0:T(8,128)(2,1)S(1)} %bitcast.9, f32[16,1,1280]{2,1,0:T(1,128)S(1)} %all_to_all.64.got), custom_call_target="tpu_custom_call" | custom-call | flops 805306368 | bytes 9437184 | tf_op jit(solution)/shard_map/pallas_call | solution.py:324
  (10 shorter events, 0.7 us)
Async XLA Ops:
  24.2 40.2 %all-to-all-start.1 = ((bf16[16,16,1024]{2,1,0:T(8,128)(2,1)}), bf16[16,16,1024]{2,1,0:T(8,128)(2,1)S(1)}, u32[]{:S(2)}, u32[]{:S(2)}) async-start(bf16[16,16,1024]{2,1,0:T(8,128)(2,1)} %get-tuple-element.20), calls=%async_computation.1 | async-start | bytes 1048576 | tf_op jit(solution)/shard_map/all_to_all | solution.py:23
  42.7 35.6 %all-gather.5.cloned.1.call-start = ((), (), s32[]{:S(2)}) async-start(), calls=%async_computation.11 | async-start | bytes 1179648 | tf_op jit(solution)/shard_map/all_gather | solution.py:261
  43.5 150.1 %all-gather.7.cloned.1.call-start = ((), (), s32[]{:S(2)}) async-start(), calls=%async_computation.12 | async-start | bytes 4718592 | tf_op jit(solution)/shard_map/all_gather | solution.py:287
  193.6 13.4 %copy-start = (bf16[2048,1024]{1,0:T(8,128)(2,1)S(1)}, bf16[2048,1024]{1,0:T(8,128)(2,1)}, u32[]{:S(2)}) copy-start(bf16[2048,1024]{1,0:T(8,128)(2,1)} %all-gather.7.cloned.1.call-done) | copy-start | bytes 12582916
Sparse Core Ops, SparseCore 0:
  46.3 32.0 all-gather.4
  81.0 64.7 all-gather.6
